TPU v7x, 16 devices: a 4x2x1 block of a 4x4x8 slice. The times are simulated.
16 devices in a mesh: dp: 2 (over y, z), tp: 8 (over x, core).
Axes of the slice: x: 4, y: 2, z: 1, core: 2. Of those that a mesh axis runs over, the one named last changes fastest.
The devices are a block of a 4x4x8 slice.
Arguments:
- enc_out: bfloat16 [24, 1024, 1024], P('dp', 'tp'), parts along dimension 0
- norm_scale: bfloat16 [1024], replicated
- w_key: bfloat16 [12, 1024, 16, 64], P(None, None, 'tp')
- w_value: bfloat16 [12, 1024, 16, 64], P(None, None, 'tp')
Outputs:
- output 1: bfloat16 [12, 24, 1024, 16, 64], P(None, 'dp', None, 'tp'), parts along dimension 1
- output 2: bfloat16 [12, 24, 1024, 16, 64], P(None, 'dp', None, 'tp'), parts along dimension 1
There are 2 independent parts. A program takes and returns all parts, laid end to end along the dimension named above; an argument that names none is the same for every part.
All inputs are finite; a program needn't handle non-finite values.
Results may differ from a plain program's by a relative error of at most 0.001.
Values are sent between devices in bfloat16 or wider.
A program may use at most 768 MiB of HBM per device.

v0:
```python
import jax
import jax.numpy as jnp
from jax import lax
from jax.sharding import PartitionSpec as P

NORM_EPS = 1e-6


def rms_norm(enc_out, norm_scale):
    acts = enc_out.astype(jnp.float32)
    mean_sq = jnp.mean(acts * acts, axis=-1, keepdims=True)
    return (acts * lax.rsqrt(mean_sq + NORM_EPS) * norm_scale.astype(jnp.float32)).astype(jnp.bfloat16)


def solution(mesh):
    def per_device(enc_out, norm_scale, w_key, w_value):
        normed = rms_norm(enc_out, norm_scale)
        gathered = lax.all_gather(normed, "tp", axis=1, tiled=True)
        key_cache = jnp.einsum("bsd,ldhk->lbshk", gathered, w_key, preferred_element_type=jnp.float32).astype(jnp.bfloat16)
        value_cache = jnp.einsum("bsd,ldhk->lbshk", gathered, w_value, preferred_element_type=jnp.float32).astype(jnp.bfloat16)
        return key_cache, value_cache

    weight_spec = P(None, None, "tp", None)
    cache_spec = P(None, "dp", None, "tp", None)
    return jax.shard_map(per_device, mesh=mesh, in_specs=(P("dp", "tp", None), P(None), weight_spec, weight_spec), out_specs=(cache_spec, cache_spec), check_vma=False)
```

profile of v0, /device:TPU:113, one launch (start us, length us, event | category | flops | bytes accessed | tf_op | source)
XLA Modules:
  0.0 347.1 jit_solution(1548432757681685522)
XLA Ops:
  7.2 0.0 copy-start
  7.2 0.1 all-gather.2.cloned.1.call-start
  7.3 0.8 convert_element_type.22
  8.1 2.6 fusion.8
  10.7 4.3 %fusion.10 = bf16[12,128,1024]{2,1,0:T(8,128)(2,1)} fusion(bf16[12,128,1024]{2,1,0:T(8,128)(2,1)} %param.4, f32[1024]{0:T(1024)S(1)} %convert_element_type.22, f32[12,128]{1,0:T(8,128)S(1)} %add_rsqrt_fusion), kind=kLoop, calls=%fused_computation.10 | loop fusion | flops 6291456 | bytes 6301696 | tf_op jit(solution)/shard_map/convert_element_type | solution.py:12
  15.1 0.1 all-gather.2.cloned.1.call-update
  15.1 120.2 %all-gather.2.cloned.1.call-done = bf16[12,1024,1024]{2,1,0:T(8,128)(2,1)} async-done(((bf16[12,128,1024]{2,1,0:T(8,128)(2,1)}), bf16[12,1024,1024]{2,1,0:T(8,128)(2,1)}) %all-gather.2.cloned.1.call-update) | async-done | bytes 25165840 | tf_op jit(solution)/shard_map/all_gather | solution.py:18
  135.3 0.0 copy-done
  135.3 76.4 %convert_bitcast_fusion = bf16[12,12,1024,2,64]{2,4,3,0,1:T(8,128)(2,1)} fusion(bf16[12,1024,1024]{2,1,0:T(8,128)(2,1)} %all-gather.2.cloned.1.call-done, bf16[12,1024,2,64]{1,3,2,0:T(8,128)(2,1)S(1)} %copy-done), kind=kOutput, calls=%fused_computation | convolution fusion | flops 38673580032 | bytes 66060288 | tf_op jit(solution)/shard_map/bsd,ldhk->lbshk/dot_general | solution.py:20
  211.8 0.0 copy-start.2
  211.8 25.1 %copy.7 = bf16[12,12,1024,2,64]{2,4,3,1,0:T(8,128)(2,1)} copy(bf16[12,12,1024,2,64]{2,4,3,0,1:T(8,128)(2,1)} %convert_bitcast_fusion) | data formatting | bytes 75497472
  236.9 0.9 copy-done.2
  237.8 76.4 %convert_bitcast_fusion.1 = bf16[12,12,1024,2,64]{2,4,3,0,1:T(8,128)(2,1)} fusion(bf16[12,1024,1024]{2,1,0:T(8,128)(2,1)} %all-gather.2.cloned.1.call-done, bf16[12,1024,2,64]{1,3,2,0:T(8,128)(2,1)S(1)} %copy-done.2), kind=kOutput, calls=%fused_computation.1 | convolution fusion | flops 38673580032 | bytes 66060288 | tf_op jit(solution)/shard_map/bsd,ldhk->lbshk/dot_general | solution.py:19
  314.2 0.0 copy-start.1
  314.2 25.1 %copy.6 = bf16[12,12,1024,2,64]{2,4,3,1,0:T(8,128)(2,1)} copy(bf16[12,12,1024,2,64]{2,4,3,0,1:T(8,128)(2,1)} %convert_bitcast_fusion.1) | data formatting | bytes 75497472
  339.3 0.9 copy-done.1
  (1 shorter events, 0.0 us)
Async XLA Ops:
  7.2 128.2 %copy-start = (bf16[12,1024,2,64]{1,3,2,0:T(8,128)(2,1)S(1)}, bf16[12,1024,2,64]{1,3,2,0:T(8,128)(2,1)}, u32[]{:S(2)}) copy-start(bf16[12,1024,2,64]{1,3,2,0:T(8,128)(2,1)} %param.7) | copy-start | bytes 9437188
  7.2 128.1 %all-gather.2.cloned.1.call-start = ((), (), s32[]{:S(2)}) async-start(), calls=%async_computation | async-start | bytes 28311552 | tf_op jit(solution)/shard_map/all_gather | solution.py:18
  211.8 26.0 %copy-start.2 = (bf16[12,1024,2,64]{1,3,2,0:T(8,128)(2,1)S(1)}, bf16[12,1024,2,64]{1,3,2,0:T(8,128)(2,1)}, u32[]{:S(2)}) copy-start(bf16[12,1024,2,64]{1,3,2,0:T(8,128)(2,1)} %param.6) | copy-start | bytes 9437188
  314.2 26.0 %copy-start.1 = (bf16[12,1024,2,64]{1,3,2,0:T(8,128)(2,1)S(1)}, bf16[12,1024,2,64]{1,3,2,0:T(8,128)(2,1)}, u32[]{:S(2)}) copy-start(bf16[12,1024,2,64]{1,3,2,0:T(8,128)(2,1)} %param.7) | copy-start | bytes 9437188
Sparse Core Ops, SparseCore 0:
  15.3 120.0 all-gather.1
where the time goes:
time: 347 us
  matrix products  153 us (44%)
  waiting for transfers between devices  120 us (35%)
  local copies, waits for them, and re-layouts  52.1 us (15%)
  between operations  14.1 us (4%)
  other arithmetic  7.8 us (2%)
    all_gather x1, waiting for transfers between devices, per_device(): gathered = lax.all_gather(normed, 'tp', axis=1, tiled=True)  120 us
    dot_general x1, matrix products, per_device(): jnp.einsum('bsd,ldhk->lbshk', gathered, w_value, preferred_element_type=j...  76.4 us
    dot_general x1, matrix products, per_device(): jnp.einsum('bsd,ldhk->lbshk', gathered, w_key, preferred_element_type=jnp...  76.4 us
    unnamed x8, local copies, waits for them, and re-layouts  52.1 us
  transfers between devices with their start and end apart: 1, of which 1 were waited for; matrix products, arithmetic and copies ran while one was open for 0% of the time, Pallas kernels for 0%

commit v1 on v0

v1 whole, which is shorter than its diff:
```python
import functools

import jax
import jax.numpy as jnp
from jax import lax
from jax.experimental import pallas as pl
from jax.experimental.pallas import tpu as pltpu
from jax.sharding import PartitionSpec as P


NORM_EPS = 1e-6
MIB = 1024 * 1024
N_FLOPS = 8
ANY, VMEM = (pl.BlockSpec(memory_space=space) for space in (pl.ANY, pltpu.VMEM))

ORDER = (
    "n0", "m0", "n1", "m1", "m2", "sp0", "sp1", "sp2", "n_0", "n_1", "n_2",
    ("p0", "p1", "p2"),
    "fm0", "sm0",
    ("sp0", "sp1", "sp2", "m0"),
    "sn0", "fm1", "sm1",
    ("sm0", "n_0", "m1"),
    "sn1",
    ("sn0", "sm1", "n_1"),
    "fm2", "sm2",
    ("sn1", "m2"),
    "sn2",
    ("sm2", "n_2"),
    "sfm0",
    ("sn2", "fm0"),
    "sfm1",
    ("sfm0", "fm1"),
    ("sfm1",),
    "sfm2",
    ("fm2",),
    ("sfm2",),
)


def source(name):
    if name[0] == "s":
        inner = name[1:]
        return "n_" + inner[1:] if inner[0] == "n" else inner
    return name[1:] if name[0] == "f" else "p" + name[-1]


def norm(x, scale):
    acts = x.astype(jnp.float32)
    mean_sq = jnp.mean(acts * acts, axis=-1, keepdims=True)
    return (acts * lax.rsqrt(mean_sq + NORM_EPS) * scale).astype(jnp.bfloat16)


def norm_kernel(first, n_w, x_ref, scale_ref, *refs):
    weights = [pltpu.make_async_copy(refs[i], refs[-1 - n_w + i], refs[-1].at[i]) for i in range(n_w)]
    for copy in weights:
        copy.start()
    scale = scale_ref[...].astype(jnp.float32).reshape(1, -1)
    for out_ref in refs[n_w:len(refs) - 1 - n_w]:
        count = out_ref.shape[0]
        for b in range(count):
            out_ref[b] = norm(x_ref[first + b], scale)
        first += count
    for copy in weights:
        copy.wait()


def norm_pieces(enc_out, norm_scale, first, counts, weights):
    tokens, depth = enc_out.shape[1:]
    work = sum(counts) * tokens * depth
    return pl.pallas_call(
        functools.partial(norm_kernel, first, len(weights)),
        in_specs=[VMEM, VMEM] + [ANY] * len(weights),
        out_specs=[VMEM] * (len(counts) + len(weights)),
        out_shape=[jax.ShapeDtypeStruct((count, tokens, depth), jnp.bfloat16) for count in counts] + [jax.ShapeDtypeStruct(w.shape, w.dtype) for w in weights],
        scratch_shapes=[pltpu.SemaphoreType.DMA((2,))],
        compiler_params=pltpu.CompilerParams(vmem_limit_bytes=5 * MIB),
        cost_estimate=pl.CostEstimate(flops=work * N_FLOPS, bytes_accessed=work * 4, transcendentals=0),
    )(enc_out, norm_scale, *weights)


def project_kernel(pieces, group, slot0, before, last, *refs):
    n_x = len(pieces)
    x_refs, (wk_ref, wv_ref) = refs[:n_x], refs[n_x:n_x + 2]
    k_ref, v_ref, o_buf, _, _, x_buf, x_sem, o_sem = refs[-8:]
    layers, heads = k_ref.shape[0], k_ref.shape[2]
    tokens, depth = x_refs[0].shape[1:]
    me = lax.axis_index("tp")
    n_tp = lax.axis_size("tp")
    starts = [sum(rows for rows, _, _, _ in pieces[:p]) for p in range(n_x)]
    steps = sum(rows for rows, _, _, _ in pieces) // group
    far = [p for p in range(n_x) if pieces[p][3]]

    def x_copy(p):
        return pltpu.make_async_copy(x_refs[p], x_buf.at[pl.ds(starts[p], pieces[p][0])], x_sem.at[p])

    for p in far:
        x_copy(p).start()

    def owner_of(hop, flip):
        odd = lax.rem(me, 2)
        base = me + flip * (1 - 2 * odd)
        return lax.rem(base + 2 * hop * (2 * lax.rem(base, 2) - 1) + 2 * n_tp, n_tp)

    def place(block):
        seq = jnp.int32(0)
        owner = jnp.int32(0)
        for start, (rows, first, whose, _) in zip(starts, pieces):
            inside = block >= start
            seq = jnp.where(inside, first + block - start, seq)
            owner = jnp.where(inside, owner_of(*whose), owner)
        return seq, owner

    def o_copy(slot, w, g, seq, owner, results=o_buf):
        lanes = pl.ds(pl.multiple_of(owner * tokens, tokens), tokens)
        return pltpu.make_async_copy(results.at[slot, g, w], (k_ref, v_ref)[w].at[:, seq, :, lanes], o_sem.at[slot, g, w])

    def send(slot, where):
        for g, (seq, owner) in enumerate(where):
            for w in range(2):
                o_copy(slot, w, g, seq, owner).start()

    def wait(slot, count):
        for g in range(count):
            for w in range(2):
                o_copy(slot, w, g, 0, 0).wait()

    if before:
        for g, (seq, whose) in enumerate(before):
            for w in range(2):
                o_copy((slot0 + 1) % 2, w, g, seq, owner_of(*whose), refs[n_x + 4]).start()

    def step(s, carry):
        slot = lax.rem(s + slot0, 2)
        if before and steps > 1:
            @pl.when(s == 1)
            def _():
                wait((slot0 + 1) % 2, len(before))
        if steps > 2:
            @pl.when(s >= 2)
            def _():
                wait(slot, group)

        if n_x == 1 and not far:
            x = x_refs[0][pl.ds(group * s, group)]
        else:
            for p, x_ref in enumerate(x_refs):
                rows = pl.ds(starts[p], pieces[p][0])

                @pl.when(s == starts[p] // group)
                def _(p=p, x_ref=x_ref, rows=rows):
                    if p in far:
                        x_copy(p).wait()
                    else:
                        x_buf[rows] = x_ref[...]
            x = x_buf[pl.ds(group * s, group)]
        x = x.reshape(group * tokens, depth)
        chunk = 4
        for w, w_ref in enumerate((wk_ref, wv_ref)):
            for layer in range(0, layers, chunk):
                rows = w_ref[layer * heads:(layer + chunk) * heads, :]
                acc = lax.dot_general(rows, x, (((1,), (1,)), ((), ())), preferred_element_type=jnp.float32)
                acc = acc.astype(jnp.bfloat16).reshape(chunk, heads, group * tokens)
                for g in range(group):
                    o_buf[slot, g, w, layer:layer + chunk] = acc[:, :, g * tokens:(g + 1) * tokens]

        where = [place(group * s + g) for g in range(group)]
        if last:
            send(slot, where)
        elif steps > 1:
            @pl.when(s < steps - 1)
            def _():
                send(slot, where)
        return carry

    if steps == 1:
        step(0, 0)
    else:
        lax.fori_loop(0, steps, step, 0)
    if steps > 1:
        wait((slot0 + steps) % 2, group)
    elif before:
        wait((slot0 + 1) % 2, len(before))
    if last:
        wait((slot0 + steps - 1) % 2, group)


def project(pieces, state, shapes, slot0, before, last):
    cache, hold = shapes
    arrays = [piece[0] for piece in pieces]
    layout = [(x.shape[0], seq, whose, far) for x, seq, whose, far in pieces]
    total = sum(x.shape[0] for x in arrays)
    group = 4 if total >= 8 else 2
    tokens, depth = arrays[0].shape[1:]
    old, weights = state[:-2], state[-2:]
    operands = [*arrays, *weights, *old]
    n_x = len(arrays)
    aliases = {n_x: 3, n_x + 1: 4}
    if old:
        aliases.update({n_x + 2 + i: i for i in range(3)})
    staged = total if n_x > 1 or layout[0][3] else 1
    state = pl.pallas_call(
        functools.partial(project_kernel, layout, group, slot0, before, last),
        in_specs=[ANY if far else VMEM for _, _, _, far in layout] + [VMEM] * 2 + [ANY, ANY, VMEM][:len(old)],
        out_specs=[ANY, ANY, VMEM, VMEM, VMEM],
        out_shape=[cache, cache, hold, *(jax.ShapeDtypeStruct(w.shape, w.dtype) for w in weights)],
        input_output_aliases=aliases,
        scratch_shapes=[pltpu.VMEM((staged, tokens, depth), jnp.bfloat16), pltpu.SemaphoreType.DMA((n_x,)), pltpu.SemaphoreType.DMA((2, 4, 2))],
        compiler_params=pltpu.CompilerParams(vmem_limit_bytes=6 * MIB),
        cost_estimate=pl.CostEstimate(flops=total * tokens * depth, bytes_accessed=total * tokens * depth, transcendentals=0),
    )(*operands)
    blocks = [(first + r, whose) for rows, first, whose, _ in layout for r in range(rows)]
    return state, (slot0 + total // group) % 2, blocks[-group:]


def solution(mesh):
    n_tp = mesh.shape["tp"]
    perms = {
        "m": [(t, (t + 2 - 4 * (t % 2)) % n_tp) for t in range(n_tp)],
        "n": [(t, (t - 2 + 4 * (t % 2)) % n_tp) for t in range(n_tp)],
        "s": [(t, t ^ 1) for t in range(n_tp)],
    }
    hops = {"m": 1, "n": -1, "s": 0}

    def body(enc_out, norm_scale, w_key, w_value):
        layers, depth, n_heads, head_dim = w_key.shape
        n_seqs, tokens, _ = enc_out.shape
        heads = n_heads * head_dim
        third = n_seqs // 3
        wk = w_key.transpose(0, 2, 3, 1).reshape(layers * heads, depth)
        wv = w_value.transpose(0, 2, 3, 1).reshape(layers * heads, depth)
        cache = jax.ShapeDtypeStruct((layers, n_seqs, heads, tokens * n_tp), jnp.bfloat16)
        hold = jax.ShapeDtypeStruct((2, 4, 2, layers, heads, tokens), jnp.bfloat16)

        pieces = {}
        home = (0, 0)
        weights = state = before = None
        slot = 0
        for i, op in enumerate(ORDER):
            if op in ("n0", "n1"):
                count = 1 + int(op[-1])
                done = len(pieces) and 1
                made = norm_pieces(enc_out, norm_scale, third * done, [third] * count, (wk, wv) if done else ())
                if done:
                    *made, w_key, w_value = made
                    weights = (w_key, w_value)
                for part, x in enumerate(made, done):
                    pieces[f"p{part}"] = (x, third * part, home, False)
            elif isinstance(op, tuple):
                last = i == len(ORDER) - 1
                state, slot, before = project([pieces[name] for name in op], state or weights, (cache, hold), slot, before, last)
            else:
                way = "m" if op[0] == "f" else op[0]
                x, seq, (hop, flip), _ = pieces[source(op)]
                x = lax.ppermute(x, "tp", perms[way])
                pieces[op] = (x, seq, (hop + hops[way], flip + (way == "s")), way != "s")

        def leave(out):
            return out.reshape(layers, n_seqs, n_heads, head_dim, tokens * n_tp).transpose(0, 1, 4, 2, 3)

        return leave(state[0]), leave(state[1])

    weight_spec = P(None, None, "tp", None)
    cache_spec = P(None, "dp", None, "tp", None)
    return jax.shard_map(body, mesh=mesh, in_specs=(P("dp", "tp", None), P(None), weight_spec, weight_spec), out_specs=(cache_spec, cache_spec), check_vma=False)
```

time: 347 us -> 217 us (0.63)
  matrix products: 153 us -> 0 us
  Pallas kernels: 0 us -> 97 us
  local copies, waits for them, and re-layouts: 52.1 us -> 6.34 us
  waiting for transfers between devices: 120 us -> 85.3 us
  starting transfers between devices: 0.06 us -> 26.7 us
  between operations: 14.1 us -> 0.98 us
  other arithmetic: 7.8 us -> 0 us
    dot_general x2 -> x0, matrix products: 153 us -> none  [the longest x1 76.4 us: per_device(): jnp.einsum('bsd,ldhk->lbshk', gathered, w_value, preferred_element_type=j...]
    all_gather x1 -> x0, waiting for transfers between devices: 120 us -> none  [per_device(): gathered = lax.all_gather(normed, 'tp', axis=1, tiled=True)]
    pallas_call x0 -> x13, Pallas kernels: none -> 97 us  [the longest x11 95.4 us: project(): pl.pallas_call(functools.partial(project_kernel, layout, group, slot0, be...]
    ppermute x0 -> x21, waiting for transfers between devices: none -> 85.3 us  [body(): x = lax.ppermute(x, 'tp', perms[way])]
    unnamed x8, local copies, waits for them, and re-layouts: 52.1 us -> 6.34 us
    ppermute x0 -> x21, starting transfers between devices: none -> 26.7 us  [body(): x = lax.ppermute(x, 'tp', perms[way])]
    convert_element_type x2 -> x0, other arithmetic: 5.17 us -> none  [the longest x1 4.34 us: rms_norm(): (acts * lax.rsqrt(mean_sq + NORM_EPS) * norm_scale.astype(jnp.float32)).a...]
  transfers between devices with their start and end apart: 1 -> 21, of which waited for: 1 -> 8; matrix products, arithmetic and copies ran while one was open for 0% -> 0% of each run, Pallas kernels for 0% -> 41%
where the time goes in v1:
time: 217 us; the launch traced here: 216 us
  Pallas kernels  97 us (45%)
  waiting for transfers between devices  85.3 us (39%)
  starting transfers between devices  26.7 us (12%)
  local copies, waits for them, and re-layouts  6.34 us (3%)
    pallas_call x11, Pallas kernels, project(): pl.pallas_call(functools.partial(project_kernel, layout, group, slot0, be...  95.4 us
    ppermute x21, waiting for transfers between devices, body(): x = lax.ppermute(x, 'tp', perms[way])  85.3 us
    ppermute x21, starting transfers between devices, body(): x = lax.ppermute(x, 'tp', perms[way])  26.7 us
    unnamed x8, local copies, waits for them, and re-layouts  6.34 us
  transfers between devices with their start and end apart: 21, of which 8 were waited for; matrix products, arithmetic and copies ran while one was open for 0% of the time, Pallas kernels for 41%

profile of v1, /device:TPU:113, one launch (start us, length us, event | category | flops | bytes accessed | tf_op | source)
XLA Modules:
  0.0 216.3 jit_solution(16673952666215533350)
XLA Ops:
  0.6 0.0 copy-start
  0.6 1.9 copy-done
  2.5 0.0 copy-start.1
  2.5 1.9 copy-done.1
  4.4 0.0 copy-start.2
  4.4 1.9 copy-done.2
  6.3 0.0 copy-start.3
  6.3 0.7 copy-done.3
  7.0 1.2 shard_map.59
  8.2 0.8 collective-permute-start.19
  9.0 0.1 collective-permute-start.20
  9.1 0.4 shard_map.60.refs_0_
  9.5 3.7 %collective-permute-start.6 = (bf16[4,128,1024]{2,1,0:T(8,128)(2,1)S(1)}, bf16[4,128,1024]{2,1,0:T(8,128)(2,1)S(1)}, u32[]{:S(2)}, u32[]{:S(2)}) collective-permute-start(bf16[4,128,1024]{2,1,0:T(8,128)(2,1)S(1)} %shard_map.60.refs_0_), channel_id=1, source_target_pairs={{0,2},{1,7},{2,4},{3,1},{4,6},{5,3},{6,0},{7,5},{8,10},{9,15},{10,... | collective-permute-start | bytes 3145736 | tf_op jit(solution)/shard_map/ppermute | solution.py:254
  13.2 0.0 collective-permute-start.18
  13.2 0.5 collective-permute-start.3
  13.7 0.0 collective-permute-done.19.refs_1_
  13.7 1.0 collective-permute-start.14
  14.7 0.0 collective-permute-done.20.refs_2_
  14.7 0.5 collective-permute-start.12
  15.2 17.1 %collective-permute-done.6.refs_3_ = bf16[4,128,1024]{2,1,0:T(8,128)(2,1)S(1)} collective-permute-done((bf16[4,128,1024]{2,1,0:T(8,128)(2,1)S(1)}, bf16[4,128,1024]{2,1,0:T(8,128)(2,1)S(1)}, u32[]{:S(2)}, u32[]{:S(2)}) %collective-permute-start.6) | collective-permute-done | bytes 1048608 | tf_op jit(solution)/shard_map/ppermute | solution.py:254
  32.3 3.4 %collective-permute-start = (bf16[4,128,1024]{2,1,0:T(8,128)(2,1)S(1)}, bf16[4,128,1024]{2,1,0:T(8,128)(2,1)S(1)}, u32[]{:S(2)}, u32[]{:S(2)}) collective-permute-start(bf16[4,128,1024]{2,1,0:T(8,128)(2,1)S(1)} %get-tuple-element.58.refs_2_), channel_id=1, source_target_pairs={{0,2},{1,7},{2,4},{3,1},{4,6},{5,3},{6,0},{7,5},{8,10},{9,15},{10,... | collective-permute-start | bytes 3145736 | tf_op jit(solution)/shard_map/ppermute | solution.py:254
  35.7 0.0 collective-permute-done.18.refs_0_
  35.7 0.0 collective-permute-start.9
  35.7 19.1 %collective-permute-done.3.refs_2_ = bf16[4,128,1024]{2,1,0:T(8,128)(2,1)S(1)} collective-permute-done((bf16[4,128,1024]{2,1,0:T(8,128)(2,1)S(1)}, bf16[4,128,1024]{2,1,0:T(8,128)(2,1)S(1)}, u32[]{:S(2)}, u32[]{:S(2)}) %collective-permute-start.3) | collective-permute-done | bytes 1048608 | tf_op jit(solution)/shard_map/ppermute | solution.py:254
  54.7 3.1 %collective-permute-start.17 = (bf16[4,128,1024]{2,1,0:T(8,128)(2,1)S(1)}, bf16[4,128,1024]{2,1,0:T(8,128)(2,1)S(1)}, u32[]{:S(2)}, u32[]{:S(2)}) collective-permute-start(bf16[4,128,1024]{2,1,0:T(8,128)(2,1)S(1)} %collective-permute-done.6.refs_3_), channel_id=1, source_target_pairs={{0,1},{1,0},{2,3},{3,2},{4,5},{5,4},{6,7},{7,6},{8,9},{9,8},{10,11... | collective-permute-start | bytes 3145736 | tf_op jit(solution)/shard_map/ppermute | solution.py:254
  57.8 0.0 collective-permute-done.14.refs_1_
  57.8 0.0 collective-permute-start.16
  57.8 4.7 %collective-permute-done.12.refs_2_ = bf16[4,128,1024]{2,1,0:T(8,128)(2,1)S(1)} collective-permute-done((bf16[4,128,1024]{2,1,0:T(8,128)(2,1)S(1)}, bf16[4,128,1024]{2,1,0:T(8,128)(2,1)S(1)}, u32[]{:S(2)}, u32[]{:S(2)}) %collective-permute-start.12) | collective-permute-done | bytes 1048608 | tf_op jit(solution)/shard_map/ppermute | solution.py:254
  62.6 0.4 collective-permute-start.15
  63.0 14.2 %collective-permute-done.refs_1_ = bf16[4,128,1024]{2,1,0:T(8,128)(2,1)S(1)} collective-permute-done((bf16[4,128,1024]{2,1,0:T(8,128)(2,1)S(1)}, bf16[4,128,1024]{2,1,0:T(8,128)(2,1)S(1)}, u32[]{:S(2)}, u32[]{:S(2)}) %collective-permute-start) | collective-permute-done | bytes 1048608 | tf_op jit(solution)/shard_map/ppermute | solution.py:254
  77.2 3.1 %collective-permute-start.13 = (bf16[4,128,1024]{2,1,0:T(8,128)(2,1)S(1)}, bf16[4,128,1024]{2,1,0:T(8,128)(2,1)S(1)}, u32[]{:S(2)}, u32[]{:S(2)}) collective-permute-start(bf16[4,128,1024]{2,1,0:T(8,128)(2,1)S(1)} %collective-permute-done.12.refs_2_), channel_id=1, source_target_pairs={{0,1},{1,0},{2,3},{3,2},{4,5},{5,4},{6,7},{7,6},{8,9},{9,8},{10,11... | collective-permute-start | bytes 3145736 | tf_op jit(solution)/shard_map/ppermute | solution.py:254
  80.3 1.9 collective-permute-done.9.refs_1_
  82.2 2.0 collective-permute-start.7
  84.2 0.0 collective-permute-done.17.refs_0_
  84.2 0.1 collective-permute-start.4
  84.3 0.0 collective-permute-done.16.refs_1_
  84.3 0.1 collective-permute-start.1
  84.5 0.0 collective-permute-done.15.refs_0_
  84.5 2.2 %collective-permute-start.11 = (bf16[4,128,1024]{2,1,0:T(8,128)(2,1)S(1)}, bf16[4,128,1024]{2,1,0:T(8,128)(2,1)S(1)}, u32[]{:S(2)}, u32[]{:S(2)}) collective-permute-start(bf16[4,128,1024]{2,1,0:T(8,128)(2,1)S(1)} %collective-permute-done.refs_1_), channel_id=1, source_target_pairs={{0,1},{1,0},{2,3},{3,2},{4,5},{5,4},{6,7},{7,6},{8,9},{9,8},{10,11... | collective-permute-start | bytes 3145736 | tf_op jit(solution)/shard_map/ppermute | solution.py:254
  86.7 0.0 collective-permute-done.13.refs_0_
  86.7 0.1 collective-permute-start.10
  86.7 9.5 %collective-permute-done.7.refs_1_ = bf16[4,128,1024]{2,1,0:T(8,128)(2,1)} collective-permute-done((bf16[4,128,1024]{2,1,0:T(8,128)(2,1)S(1)}, bf16[4,128,1024]{2,1,0:T(8,128)(2,1)}, u32[]{:S(2)}, u32[]{:S(2)}) %collective-permute-start.7) | collective-permute-done | bytes 1048608 | tf_op jit(solution)/shard_map/ppermute | solution.py:254
  96.2 1.9 collective-permute-start.8
  98.1 9.4 %collective-permute-done.4.refs_1_ = bf16[4,128,1024]{2,1,0:T(8,128)(2,1)} collective-permute-done((bf16[4,128,1024]{2,1,0:T(8,128)(2,1)S(1)}, bf16[4,128,1024]{2,1,0:T(8,128)(2,1)}, u32[]{:S(2)}, u32[]{:S(2)}) %collective-permute-start.4) | collective-permute-done | bytes 1048608 | tf_op jit(solution)/shard_map/ppermute | solution.py:254
  107.5 1.9 collective-permute-start.5
  109.3 9.4 %collective-permute-done.1.refs_0_ = bf16[4,128,1024]{2,1,0:T(8,128)(2,1)} collective-permute-done((bf16[4,128,1024]{2,1,0:T(8,128)(2,1)S(1)}, bf16[4,128,1024]{2,1,0:T(8,128)(2,1)}, u32[]{:S(2)}, u32[]{:S(2)}) %collective-permute-start.1) | collective-permute-done | bytes 1048608 | tf_op jit(solution)/shard_map/ppermute | solution.py:254
  118.7 1.9 collective-permute-start.2
  120.6 10.9 %shard_map.61 = (bf16[12,12,128,1024]{3,2,1,0:T(8,128)(2,1)}, bf16[12,12,128,1024]{3,2,1,0:T(8,128)(2,1)}, bf16[2,4,2,12,128,128]{5,4,3,2,1,0:T(8,128)(2,1)S(1)}...) custom-call(bf16[4,128,1024]{2,1,0:T(8,128)(2,1)S(1)} %shard_map.60.refs_0_, ...), custom_call_target="tpu_custom_call", output_to_operand_aliasing={{3}: (3, {}), {4}: (4, {})} | custom-call | flops 1572864 | bytes 1572864 | tf_op jit(solution)/shard_map/pallas_call | solution.py:201
  131.5 14.7 %shard_map.62 = (bf16[12,12,128,1024]{3,2,1,0:T(8,128)(2,1)}, bf16[12,12,128,1024]{3,2,1,0:T(8,128)(2,1)}, bf16[2,4,2,12,128,128]{5,4,3,2,1,0:T(8,128)(2,1)S(1)}...) custom-call(bf16[4,128,1024]{2,1,0:T(8,128)(2,1)S(1)} %collective-pe, ...), custom_call_target="tpu_custom_call", output_to_operand_aliasing={{3}: (4, {}), {4}: (5, {}), {0}: (6, {}), {1}: (7, {}), {2}... | custom-call | flops 2097152 | bytes 2097152 | tf_op jit(solution)/shard_map/pallas_call | solution.py:201
  146.2 11.0 %shard_map.63 = (bf16[12,12,128,1024]{3,2,1,0:T(8,128)(2,1)}, bf16[12,12,128,1024]{3,2,1,0:T(8,128)(2,1)}, bf16[2,4,2,12,128,128]{5,4,3,2,1,0:T(8,128)(2,1)S(1)}...) custom-call(bf16[4,128,1024]{2,1,0:T(8,128)(2,1)S(1)} %collective-pe, ...), custom_call_target="tpu_custom_call", output_to_operand_aliasing={{3}: (3, {}), {4}: (4, {}), {0}: (5, {}), {1}: (6, {}), {2}... | custom-call | flops 1572864 | bytes 1572864 | tf_op jit(solution)/shard_map/pallas_call | solution.py:201
  157.2 11.2 %shard_map.64 = (bf16[12,12,128,1024]{3,2,1,0:T(8,128)(2,1)}, bf16[12,12,128,1024]{3,2,1,0:T(8,128)(2,1)}, bf16[2,4,2,12,128,128]{5,4,3,2,1,0:T(8,128)(2,1)S(1)}...) custom-call(bf16[4,128,1024]{2,1,0:T(8,128)(2,1)S(1)} %collective-pe, ...), custom_call_target="tpu_custom_call", output_to_operand_aliasing={{3}: (3, {}), {4}: (4, {}), {0}: (5, {}), {1}: (6, {}), {2}... | custom-call | flops 1572864 | bytes 1572864 | tf_op jit(solution)/shard_map/pallas_call | solution.py:201
  168.4 7.4 %shard_map.65 = (bf16[12,12,128,1024]{3,2,1,0:T(8,128)(2,1)}, bf16[12,12,128,1024]{3,2,1,0:T(8,128)(2,1)}, bf16[2,4,2,12,128,128]{5,4,3,2,1,0:T(8,128)(2,1)S(1)}...) custom-call(bf16[4,128,1024]{2,1,0:T(8,128)(2,1)S(1)} %collective-pe, ...), custom_call_target="tpu_custom_call", output_to_operand_aliasing={{3}: (2, {}), {4}: (3, {}), {0}: (4, {}), {1}: (5, {}), {2}... | custom-call | flops 1048576 | bytes 1048576 | tf_op jit(solution)/shard_map/pallas_call | solution.py:201
  175.8 0.0 collective-permute-done.11.refs_0_
  175.9 7.4 %shard_map.66 = (bf16[12,12,128,1024]{3,2,1,0:T(8,128)(2,1)}, bf16[12,12,128,1024]{3,2,1,0:T(8,128)(2,1)}, bf16[2,4,2,12,128,128]{5,4,3,2,1,0:T(8,128)(2,1)S(1)}...) custom-call(bf16[4,128,1024]{2,1,0:T(8,128)(2,1)S(1)} %collective-pe, ...), custom_call_target="tpu_custom_call", output_to_operand_aliasing={{3}: (2, {}), {4}: (3, {}), {0}: (4, {}), {1}: (5, {}), {2}... | custom-call | flops 1048576 | bytes 1048576 | tf_op jit(solution)/shard_map/pallas_call | solution.py:201
  183.3 0.0 collective-permute-done.10.refs_0_
  183.3 7.3 %shard_map.67 = (bf16[12,12,128,1024]{3,2,1,0:T(8,128)(2,1)}, bf16[12,12,128,1024]{3,2,1,0:T(8,128)(2,1)}, bf16[2,4,2,12,128,128]{5,4,3,2,1,0:T(8,128)(2,1)S(1)}...) custom-call(bf16[4,128,1024]{2,1,0:T(8,128)(2,1)S(1)} %collective-pe, ...), custom_call_target="tpu_custom_call", output_to_operand_aliasing={{3}: (2, {}), {4}: (3, {}), {0}: (4, {}), {1}: (5, {}), {2}... | custom-call | flops 1048576 | bytes 1048576 | tf_op jit(solution)/shard_map/pallas_call | solution.py:201
  190.6 0.0 collective-permute-done.8.refs_0_
  190.6 8.5 %shard_map.68 = (bf16[12,12,128,1024]{3,2,1,0:T(8,128)(2,1)}, bf16[12,12,128,1024]{3,2,1,0:T(8,128)(2,1)}, bf16[2,4,2,12,128,128]{5,4,3,2,1,0:T(8,128)(2,1)S(1)}...) custom-call(bf16[4,128,1024]{2,1,0:T(8,128)(2,1)} %collective-permut, ...), custom_call_target="tpu_custom_call", output_to_operand_aliasing={{3}: (2, {}), {4}: (3, {}), {0}: (4, {}), {1}: (5, {}), {2}... | custom-call | flops 1048576 | bytes 1048576 | tf_op jit(solution)/shard_map/pallas_call | solution.py:201
  199.1 0.0 collective-permute-done.5.refs_0_
  199.1 5.1 %shard_map.69 = (bf16[12,12,128,1024]{3,2,1,0:T(8,128)(2,1)}, bf16[12,12,128,1024]{3,2,1,0:T(8,128)(2,1)}, bf16[2,4,2,12,128,128]{5,4,3,2,1,0:T(8,128)(2,1)S(1)}...) custom-call(bf16[4,128,1024]{2,1,0:T(8,128)(2,1)} %collective-permut, ...), custom_call_target="tpu_custom_call", output_to_operand_aliasing={{3}: (1, {}), {4}: (2, {}), {0}: (3, {}), {1}: (4, {}), {2}... | custom-call | flops 524288 | bytes 524288 | tf_op jit(solution)/shard_map/pallas_call | solution.py:201
  204.2 5.6 %shard_map.70 = (bf16[12,12,128,1024]{3,2,1,0:T(8,128)(2,1)}, bf16[12,12,128,1024]{3,2,1,0:T(8,128)(2,1)}, bf16[2,4,2,12,128,128]{5,4,3,2,1,0:T(8,128)(2,1)S(1)}...) custom-call(bf16[4,128,1024]{2,1,0:T(8,128)(2,1)} %collective-permut, ...), custom_call_target="tpu_custom_call", output_to_operand_aliasing={{3}: (1, {}), {4}: (2, {}), {0}: (3, {}), {1}: (4, {}), {2}... | custom-call | flops 524288 | bytes 524288 | tf_op jit(solution)/shard_map/pallas_call | solution.py:201
  209.9 0.0 collective-permute-done.2.refs_0_
  209.9 6.2 %shard_map.71 = (bf16[12,12,128,1024]{3,2,1,0:T(8,128)(2,1)}, bf16[12,12,128,1024]{3,2,1,0:T(8,128)(2,1)}, bf16[2,4,2,12,128,128]{5,4,3,2,1,0:T(8,128)(2,1)S(1)}...) custom-call(bf16[4,128,1024]{2,1,0:T(8,128)(2,1)} %collective-permut, ...), custom_call_target="tpu_custom_call", output_to_operand_aliasing={{3}: (1, {}), {4}: (2, {}), {0}: (3, {}), {1}: (4, {}), {2}... | custom-call | flops 524288 | bytes 524288 | tf_op jit(solution)/shard_map/pallas_call | solution.py:201
Async XLA Ops:
  0.6 1.9 copy-start
  2.5 1.9 copy-start.1
  4.4 1.9 copy-start.2
  6.3 0.7 copy-start.3
  8.2 5.5 %collective-permute-start.19 = (bf16[4,128,1024]{2,1,0:T(8,128)(2,1)S(1)}, bf16[4,128,1024]{2,1,0:T(8,128)(2,1)S(1)}, u32[]{:S(2)}, u32[]{:S(2)}) collective-permute-start(bf16[4,128,1024]{2,1,0:T(8,128)(2,1)S(1)} %get-tuple-element.59.refs_1_), channel_id=1, source_target_pairs={{0,1},{1,0},{2,3},{3,2},{4,5},{5,4},{6,7},{7,6},{8,9},{9,8},{10,11... | collective-permute-start | bytes 3145736 | tf_op jit(solution)/shard_map/ppermute | solution.py:254
  9.0 5.7 %collective-permute-start.20 = (bf16[4,128,1024]{2,1,0:T(8,128)(2,1)S(1)}, bf16[4,128,1024]{2,1,0:T(8,128)(2,1)S(1)}, u32[]{:S(2)}, u32[]{:S(2)}) collective-permute-start(bf16[4,128,1024]{2,1,0:T(8,128)(2,1)S(1)} %get-tuple-element.58.refs_2_), channel_id=1, source_target_pairs={{0,1},{1,0},{2,3},{3,2},{4,5},{5,4},{6,7},{7,6},{8,9},{9,8},{10,11... | collective-permute-start | bytes 3145736 | tf_op jit(solution)/shard_map/ppermute | solution.py:254
  9.5 22.7 %collective-permute-start.6 = (bf16[4,128,1024]{2,1,0:T(8,128)(2,1)S(1)}, bf16[4,128,1024]{2,1,0:T(8,128)(2,1)S(1)}, u32[]{:S(2)}, u32[]{:S(2)}) collective-permute-start(bf16[4,128,1024]{2,1,0:T(8,128)(2,1)S(1)} %shard_map.60.refs_0_), channel_id=1, source_target_pairs={{0,2},{1,7},{2,4},{3,1},{4,6},{5,3},{6,0},{7,5},{8,10},{9,15},{10,... | collective-permute-start | bytes 3145736 | tf_op jit(solution)/shard_map/ppermute | solution.py:254
  13.2 22.5 %collective-permute-start.18 = (bf16[4,128,1024]{2,1,0:T(8,128)(2,1)S(1)}, bf16[4,128,1024]{2,1,0:T(8,128)(2,1)S(1)}, u32[]{:S(2)}, u32[]{:S(2)}) collective-permute-start(bf16[4,128,1024]{2,1,0:T(8,128)(2,1)S(1)} %shard_map.60.refs_0_), channel_id=1, source_target_pairs={{0,1},{1,0},{2,3},{3,2},{4,5},{5,4},{6,7},{7,6},{8,9},{9,8},{10,11... | collective-permute-start | bytes 3145736 | tf_op jit(solution)/shard_map/ppermute | solution.py:254
  13.2 41.5 %collective-permute-start.3 = (bf16[4,128,1024]{2,1,0:T(8,128)(2,1)S(1)}, bf16[4,128,1024]{2,1,0:T(8,128)(2,1)S(1)}, u32[]{:S(2)}, u32[]{:S(2)}) collective-permute-start(bf16[4,128,1024]{2,1,0:T(8,128)(2,1)S(1)} %get-tuple-element.59.refs_1_), channel_id=1, source_target_pairs={{0,2},{1,7},{2,4},{3,1},{4,6},{5,3},{6,0},{7,5},{8,10},{9,15},{10,... | collective-permute-start | bytes 3145736 | tf_op jit(solution)/shard_map/ppermute | solution.py:254
  13.7 44.1 %collective-permute-start.14 = (bf16[4,128,1024]{2,1,0:T(8,128)(2,1)S(1)}, bf16[4,128,1024]{2,1,0:T(8,128)(2,1)S(1)}, u32[]{:S(2)}, u32[]{:S(2)}) collective-permute-start(bf16[4,128,1024]{2,1,0:T(8,128)(2,1)S(1)} %shard_map.60.refs_0_), channel_id=1, source_target_pairs={{0,6},{1,3},{2,0},{3,5},{4,2},{5,7},{6,4},{7,1},{8,14},{9,11},{10,... | collective-permute-start | bytes 3145736 | tf_op jit(solution)/shard_map/ppermute | solution.py:254
  14.7 47.9 %collective-permute-start.12 = (bf16[4,128,1024]{2,1,0:T(8,128)(2,1)S(1)}, bf16[4,128,1024]{2,1,0:T(8,128)(2,1)S(1)}, u32[]{:S(2)}, u32[]{:S(2)}) collective-permute-start(bf16[4,128,1024]{2,1,0:T(8,128)(2,1)S(1)} %get-tuple-element.59.refs_1_), channel_id=1, source_target_pairs={{0,6},{1,3},{2,0},{3,5},{4,2},{5,7},{6,4},{7,1},{8,14},{9,11},{10,... | collective-permute-start | bytes 3145736 | tf_op jit(solution)/shard_map/ppermute | solution.py:254
  32.3 44.9 %collective-permute-start = (bf16[4,128,1024]{2,1,0:T(8,128)(2,1)S(1)}, bf16[4,128,1024]{2,1,0:T(8,128)(2,1)S(1)}, u32[]{:S(2)}, u32[]{:S(2)}) collective-permute-start(bf16[4,128,1024]{2,1,0:T(8,128)(2,1)S(1)} %get-tuple-element.58.refs_2_), channel_id=1, source_target_pairs={{0,2},{1,7},{2,4},{3,1},{4,6},{5,3},{6,0},{7,5},{8,10},{9,15},{10,... | collective-permute-start | bytes 3145736 | tf_op jit(solution)/shard_map/ppermute | solution.py:254
  35.7 46.5 %collective-permute-start.9 = (bf16[4,128,1024]{2,1,0:T(8,128)(2,1)S(1)}, bf16[4,128,1024]{2,1,0:T(8,128)(2,1)S(1)}, u32[]{:S(2)}, u32[]{:S(2)}) collective-permute-start(bf16[4,128,1024]{2,1,0:T(8,128)(2,1)S(1)} %get-tuple-element.58.refs_2_), channel_id=1, source_target_pairs={{0,6},{1,3},{2,0},{3,5},{4,2},{5,7},{6,4},{7,1},{8,14},{9,11},{10,... | collective-permute-start | bytes 3145736 | tf_op jit(solution)/shard_map/ppermute | solution.py:254
  54.7 29.5 %collective-permute-start.17 = (bf16[4,128,1024]{2,1,0:T(8,128)(2,1)S(1)}, bf16[4,128,1024]{2,1,0:T(8,128)(2,1)S(1)}, u32[]{:S(2)}, u32[]{:S(2)}) collective-permute-start(bf16[4,128,1024]{2,1,0:T(8,128)(2,1)S(1)} %collective-permute-done.6.refs_3_), channel_id=1, source_target_pairs={{0,1},{1,0},{2,3},{3,2},{4,5},{5,4},{6,7},{7,6},{8,9},{9,8},{10,11... | collective-permute-start | bytes 3145736 | tf_op jit(solution)/shard_map/ppermute | solution.py:254
  57.8 26.5 %collective-permute-start.16 = (bf16[4,128,1024]{2,1,0:T(8,128)(2,1)S(1)}, bf16[4,128,1024]{2,1,0:T(8,128)(2,1)S(1)}, u32[]{:S(2)}, u32[]{:S(2)}) collective-permute-start(bf16[4,128,1024]{2,1,0:T(8,128)(2,1)S(1)} %collective-permute-done.3.refs_2_), channel_id=1, source_target_pairs={{0,1},{1,0},{2,3},{3,2},{4,5},{5,4},{6,7},{7,6},{8,9},{9,8},{10,11... | collective-permute-start | bytes 3145736 | tf_op jit(solution)/shard_map/ppermute | solution.py:254
  62.6 21.9 %collective-permute-start.15 = (bf16[4,128,1024]{2,1,0:T(8,128)(2,1)S(1)}, bf16[4,128,1024]{2,1,0:T(8,128)(2,1)S(1)}, u32[]{:S(2)}, u32[]{:S(2)}) collective-permute-start(bf16[4,128,1024]{2,1,0:T(8,128)(2,1)S(1)} %collective-permute-done.14.refs_1_), channel_id=1, source_target_pairs={{0,1},{1,0},{2,3},{3,2},{4,5},{5,4},{6,7},{7,6},{8,9},{9,8},{10,11... | collective-permute-start | bytes 3145736 | tf_op jit(solution)/shard_map/ppermute | solution.py:254
  77.2 9.5 %collective-permute-start.13 = (bf16[4,128,1024]{2,1,0:T(8,128)(2,1)S(1)}, bf16[4,128,1024]{2,1,0:T(8,128)(2,1)S(1)}, u32[]{:S(2)}, u32[]{:S(2)}) collective-permute-start(bf16[4,128,1024]{2,1,0:T(8,128)(2,1)S(1)} %collective-permute-done.12.refs_2_), channel_id=1, source_target_pairs={{0,1},{1,0},{2,3},{3,2},{4,5},{5,4},{6,7},{7,6},{8,9},{9,8},{10,11... | collective-permute-start | bytes 3145736 | tf_op jit(solution)/shard_map/ppermute | solution.py:254
  82.2 14.0 %collective-permute-start.7 = (bf16[4,128,1024]{2,1,0:T(8,128)(2,1)S(1)}, bf16[4,128,1024]{2,1,0:T(8,128)(2,1)}, u32[]{:S(2)}, u32[]{:S(2)}) collective-permute-start(bf16[4,128,1024]{2,1,0:T(8,128)(2,1)S(1)} %collective-permute-done.6.refs_3_), channel_id=1, source_target_pairs={{0,2},{1,7},{2,4},{3,1},{4,6},{5,3},{6,0},{7,5},{8,10},{9,15},{10,... | collective-permute-start | bytes 3145736 | tf_op jit(solution)/shard_map/ppermute | solution.py:254
  84.2 23.3 %collective-permute-start.4 = (bf16[4,128,1024]{2,1,0:T(8,128)(2,1)S(1)}, bf16[4,128,1024]{2,1,0:T(8,128)(2,1)}, u32[]{:S(2)}, u32[]{:S(2)}) collective-permute-start(bf16[4,128,1024]{2,1,0:T(8,128)(2,1)S(1)} %collective-permute-done.3.refs_2_), channel_id=1, source_target_pairs={{0,2},{1,7},{2,4},{3,1},{4,6},{5,3},{6,0},{7,5},{8,10},{9,15},{10,... | collective-permute-start | bytes 3145736 | tf_op jit(solution)/shard_map/ppermute | solution.py:254
  84.3 34.4 %collective-permute-start.1 = (bf16[4,128,1024]{2,1,0:T(8,128)(2,1)S(1)}, bf16[4,128,1024]{2,1,0:T(8,128)(2,1)}, u32[]{:S(2)}, u32[]{:S(2)}) collective-permute-start(bf16[4,128,1024]{2,1,0:T(8,128)(2,1)S(1)} %collective-permute-done.refs_1_), channel_id=1, source_target_pairs={{0,2},{1,7},{2,4},{3,1},{4,6},{5,3},{6,0},{7,5},{8,10},{9,15},{10,... | collective-permute-start | bytes 3145736 | tf_op jit(solution)/shard_map/ppermute | solution.py:254
  84.5 91.4 %collective-permute-start.11 = (bf16[4,128,1024]{2,1,0:T(8,128)(2,1)S(1)}, bf16[4,128,1024]{2,1,0:T(8,128)(2,1)S(1)}, u32[]{:S(2)}, u32[]{:S(2)}) collective-permute-start(bf16[4,128,1024]{2,1,0:T(8,128)(2,1)S(1)} %collective-permute-done.refs_1_), channel_id=1, source_target_pairs={{0,1},{1,0},{2,3},{3,2},{4,5},{5,4},{6,7},{7,6},{8,9},{9,8},{10,11... | collective-permute-start | bytes 3145736 | tf_op jit(solution)/shard_map/ppermute | solution.py:254
  86.7 96.6 %collective-permute-start.10 = (bf16[4,128,1024]{2,1,0:T(8,128)(2,1)S(1)}, bf16[4,128,1024]{2,1,0:T(8,128)(2,1)S(1)}, u32[]{:S(2)}, u32[]{:S(2)}) collective-permute-start(bf16[4,128,1024]{2,1,0:T(8,128)(2,1)S(1)} %collective-permute-done.9.refs_1_), channel_id=1, source_target_pairs={{0,1},{1,0},{2,3},{3,2},{4,5},{5,4},{6,7},{7,6},{8,9},{9,8},{10,11... | collective-permute-start | bytes 3145736 | tf_op jit(solution)/shard_map/ppermute | solution.py:254
  96.2 94.4 %collective-permute-start.8 = (bf16[4,128,1024]{2,1,0:T(8,128)(2,1)}, bf16[4,128,1024]{2,1,0:T(8,128)(2,1)}, u32[]{:S(2)}, u32[]{:S(2)}) collective-permute-start(bf16[4,128,1024]{2,1,0:T(8,128)(2,1)} %collective-permute-done.7.refs_1_), channel_id=1, source_target_pairs={{0,1},{1,0},{2,3},{3,2},{4,5},{5,4},{6,7},{7,6},{8,9},{9,8},{10,11... | collective-permute-start | bytes 3145736 | tf_op jit(solution)/shard_map/ppermute | solution.py:254
  107.5 91.6 %collective-permute-start.5 = (bf16[4,128,1024]{2,1,0:T(8,128)(2,1)}, bf16[4,128,1024]{2,1,0:T(8,128)(2,1)}, u32[]{:S(2)}, u32[]{:S(2)}) collective-permute-start(bf16[4,128,1024]{2,1,0:T(8,128)(2,1)} %collective-permute-done.4.refs_1_), channel_id=1, source_target_pairs={{0,1},{1,0},{2,3},{3,2},{4,5},{5,4},{6,7},{7,6},{8,9},{9,8},{10,11... | collective-permute-start | bytes 3145736 | tf_op jit(solution)/shard_map/ppermute | solution.py:254
  118.7 91.2 %collective-permute-start.2 = (bf16[4,128,1024]{2,1,0:T(8,128)(2,1)}, bf16[4,128,1024]{2,1,0:T(8,128)(2,1)}, u32[]{:S(2)}, u32[]{:S(2)}) collective-permute-start(bf16[4,128,1024]{2,1,0:T(8,128)(2,1)} %collective-permute-done.1.refs_0_), channel_id=1, source_target_pairs={{0,1},{1,0},{2,3},{3,2},{4,5},{5,4},{6,7},{7,6},{8,9},{9,8},{10,11... | collective-permute-start | bytes 3145736 | tf_op jit(solution)/shard_map/ppermute | solution.py:254

commit v2 on v1

--- a/solution.py
+++ b/solution.py
@@ -11,21 +11,37 @@
 NORM_EPS = 1e-6
 MIB = 1024 * 1024
 N_FLOPS = 8
-ANY, VMEM = (pl.BlockSpec(memory_space=space) for space in (pl.ANY, pltpu.VMEM))
+PARTS = (4, 4, 4)
+ANY, VMEM, HBM = (pl.BlockSpec(memory_space=space) for space in (pl.ANY, pltpu.VMEM, pltpu.HBM))
 
 ORDER = (
-    "n0", "m0", "n1", "m1", "m2", "sp0", "sp1", "sp2", "n_0", "n_1", "n_2",
+    "n0",
+    "m0",
+    "n1",
+    "m1",
+    "m2",
+    "sp0",
+    "sp1",
+    "sp2",
+    "n_0",
+    "n_1",
+    "n_2",
     ("p0", "p1", "p2"),
-    "fm0", "sm0",
+    "fm0",
+    "sm0",
     ("sp0", "sp1", "sp2", "m0"),
-    "sn0", "fm1", "sm1",
-    ("sm0", "n_0", "m1"),
+    "sn0",
+    ("sm0", "n_0"),
+    "fm1",
+    "sm1",
+    ("sn0", "m1"),
     "sn1",
-    ("sn0", "sm1", "n_1"),
-    "fm2", "sm2",
-    ("sn1", "m2"),
+    ("sm1", "n_1"),
+    "fm2",
+    "sm2",
+    ("sn1", "m2", "sm2"),
     "sn2",
-    ("sm2", "n_2"),
+    ("n_2",),
     "sfm0",
     ("sn2", "fm0"),
     "sfm1",
@@ -51,15 +67,22 @@
 
 
 def norm_kernel(first, n_w, x_ref, scale_ref, *refs):
-    weights = [pltpu.make_async_copy(refs[i], refs[-1 - n_w + i], refs[-1].at[i]) for i in range(n_w)]
-    for copy in weights:
+    outs = refs[n_w:-4 - n_w]
+    x_buf, scale_buf, sem, w_sem = refs[-4:]
+    total = sum(out_ref.shape[0] for out_ref in outs)
+    copies = [pltpu.make_async_copy(x_ref.at[first + b], x_buf.at[b], sem.at[b]) for b in range(total)]
+    scale_copy = pltpu.make_async_copy(scale_ref, scale_buf, sem.at[total])
+    weights = [pltpu.make_async_copy(refs[i], refs[-4 - n_w + i], w_sem.at[i]) for i in range(n_w)]
+    for copy in (scale_copy, *copies, *weights):
         copy.start()
-    scale = scale_ref[...].astype(jnp.float32).reshape(1, -1)
-    for out_ref in refs[n_w:len(refs) - 1 - n_w]:
-        count = out_ref.shape[0]
-        for b in range(count):
-            out_ref[b] = norm(x_ref[first + b], scale)
-        first += count
+    scale_copy.wait()
+    scale = scale_buf[...].astype(jnp.float32).reshape(1, -1)
+    at = 0
+    for out_ref in outs:
+        for b in range(out_ref.shape[0]):
+            copies[at].wait()
+            out_ref[b] = norm(x_buf[at], scale)
+            at += 1
     for copy in weights:
         copy.wait()
 
@@ -69,13 +92,13 @@
     work = sum(counts) * tokens * depth
     return pl.pallas_call(
         functools.partial(norm_kernel, first, len(weights)),
-        in_specs=[VMEM, VMEM] + [ANY] * len(weights),
+        in_specs=[HBM] * (2 + len(weights)),
         out_specs=[VMEM] * (len(counts) + len(weights)),
         out_shape=[jax.ShapeDtypeStruct((count, tokens, depth), jnp.bfloat16) for count in counts] + [jax.ShapeDtypeStruct(w.shape, w.dtype) for w in weights],
-        scratch_shapes=[pltpu.SemaphoreType.DMA((2,))],
-        compiler_params=pltpu.CompilerParams(vmem_limit_bytes=5 * MIB),
+        scratch_shapes=[pltpu.VMEM((sum(counts), tokens, depth), jnp.bfloat16), pltpu.VMEM((depth,), jnp.bfloat16), pltpu.SemaphoreType.DMA((sum(counts) + 1,)), pltpu.SemaphoreType.DMA((2,))],
+        compiler_params=pltpu.CompilerParams(vmem_limit_bytes=8 * MIB),
         cost_estimate=pl.CostEstimate(flops=work * N_FLOPS, bytes_accessed=work * 4, transcendentals=0),
-    )(enc_out, norm_scale, *weights)
+    )(*(pltpu.with_memory_space_constraint(x, pltpu.HBM) for x in (enc_out, norm_scale, *weights)))
 
 
 def project_kernel(pieces, group, slot0, before, last, *refs):
@@ -189,7 +212,7 @@
     arrays = [piece[0] for piece in pieces]
     layout = [(x.shape[0], seq, whose, far) for x, seq, whose, far in pieces]
     total = sum(x.shape[0] for x in arrays)
-    group = 4 if total >= 8 else 2
+    group = 4 if total >= 8 and total % 4 == 0 else 2
     tokens, depth = arrays[0].shape[1:]
     old, weights = state[:-2], state[-2:]
     operands = [*arrays, *weights, *old]
@@ -225,7 +248,8 @@
         layers, depth, n_heads, head_dim = w_key.shape
         n_seqs, tokens, _ = enc_out.shape
         heads = n_heads * head_dim
-        third = n_seqs // 3
+        sizes = [n_seqs * part // 12 for part in PARTS]
+        firsts = [sum(sizes[:part]) for part in range(len(sizes))]
         wk = w_key.transpose(0, 2, 3, 1).reshape(layers * heads, depth)
         wv = w_value.transpose(0, 2, 3, 1).reshape(layers * heads, depth)
         cache = jax.ShapeDtypeStruct((layers, n_seqs, heads, tokens * n_tp), jnp.bfloat16)
@@ -237,14 +261,14 @@
         slot = 0
         for i, op in enumerate(ORDER):
             if op in ("n0", "n1"):
-                count = 1 + int(op[-1])
-                done = len(pieces) and 1
-                made = norm_pieces(enc_out, norm_scale, third * done, [third] * count, (wk, wv) if done else ())
+                done = int(op[-1])
+                counts = sizes[1:] if done else sizes[:1]
+                made = norm_pieces(enc_out, norm_scale, firsts[done], counts, (wk, wv) if done else ())
                 if done:
                     *made, w_key, w_value = made
                     weights = (w_key, w_value)
                 for part, x in enumerate(made, done):
-                    pieces[f"p{part}"] = (x, third * part, home, False)
+                    pieces[f"p{part}"] = (x, firsts[part], home, False)
             elif isinstance(op, tuple):
                 last = i == len(ORDER) - 1
                 state, slot, before = project([pieces[name] for name in op], state or weights, (cache, hold), slot, before, last)

time: 217 us -> 217 us (level)
  Pallas kernels: 97 us -> 104 us
  local copies, waits for them, and re-layouts: 6.34 us -> 0 us
  starting transfers between devices: 26.7 us -> 23.4 us
  waiting for transfers between devices: 85.3 us -> 88.6 us
    unnamed x8 -> x0, local copies, waits for them, and re-layouts: 6.34 us -> none
    pallas_call x2, Pallas kernels: 1.66 us -> 5.25 us  [norm_pieces(): pl.pallas_call(functools.partial(norm_kernel, first, len(weights)), in_sp...]
    pallas_call x11 -> x12, Pallas kernels: 95.4 us -> 98.8 us  [project(): pl.pallas_call(functools.partial(project_kernel, layout, group, slot0, be...]
    ppermute x21, waiting for transfers between devices: 85.3 us -> 88.6 us  [body(): x = lax.ppermute(x, 'tp', perms[way])]
    ppermute x21, starting transfers between devices: 26.7 us -> 23.4 us  [body(): x = lax.ppermute(x, 'tp', perms[way])]
  transfers between devices with their start and end apart: 21 -> 21, of which waited for: 8 -> 9; matrix products, arithmetic and copies ran while one was open for 0% -> 0% of each run, Pallas kernels for 41% -> 43%
where the time goes in v2:
time: 217 us
  Pallas kernels  104 us (48%)
  waiting for transfers between devices  88.6 us (41%)
  starting transfers between devices  23.4 us (11%)
    pallas_call x12, Pallas kernels, project(): pl.pallas_call(functools.partial(project_kernel, layout, group, slot0, be...  98.8 us
    ppermute x21, waiting for transfers between devices, body(): x = lax.ppermute(x, 'tp', perms[way])  88.6 us
    ppermute x21, starting transfers between devices, body(): x = lax.ppermute(x, 'tp', perms[way])  23.4 us
    pallas_call x2, Pallas kernels, norm_pieces(): pl.pallas_call(functools.partial(norm_kernel, first, len(weights)), in_sp...  5.25 us
  transfers between devices with their start and end apart: 21, of which 9 were waited for; matrix products, arithmetic and copies ran while one was open for 0% of the time, Pallas kernels for 43%

profile of v2, /device:TPU:113, one launch (start us, length us, event | category | flops | bytes accessed | tf_op | source)
XLA Modules:
  0.0 217.0 jit_solution(5738930376034790446)
XLA Ops:
  0.6 3.6 %shard_map.59 = (bf16[4,128,1024]{2,1,0:T(8,128)(2,1)S(1)}, bf16[4,128,1024]{2,1,0:T(8,128)(2,1)S(1)}, bf16[1536,1024]{1,0:T(8,128)(2,1)S(1)}, bf16[1536,1024]{1,0:T(8,128)(2,1)S(1)}) custom-call(bf16[12,128,1024]{2,1,0:T(8,128)(2,1)} %x_ref.3, bf16[1024]{0:T(1024)(128)(2,1)} %scale_ref.3, bf16[1536,1024]{1,0:T(8,128)(2,1)} %bitcast.14, ...), custom_call_target="tpu_custom_call" | custom-call | flops 8388608 | bytes 4194304 | tf_op jit(solution)/shard_map/pallas_call | solution.py:93
  4.2 0.8 collective-permute-start.19
  5.0 0.1 collective-permute-start.20
  5.1 1.6 shard_map.60.refs_0_
  6.8 3.7 %collective-permute-start.6 = (bf16[4,128,1024]{2,1,0:T(8,128)(2,1)S(1)}, bf16[4,128,1024]{2,1,0:T(8,128)(2,1)S(1)}, u32[]{:S(2)}, u32[]{:S(2)}) collective-permute-start(bf16[4,128,1024]{2,1,0:T(8,128)(2,1)S(1)} %shard_map.60.refs_0_), channel_id=1, source_target_pairs={{0,2},{1,7},{2,4},{3,1},{4,6},{5,3},{6,0},{7,5},{8,10},{9,15},{10,... | collective-permute-start | bytes 3145736 | tf_op jit(solution)/shard_map/ppermute | solution.py:278
  10.5 0.0 collective-permute-start.18
  10.5 0.5 collective-permute-start.15
  11.0 0.0 collective-permute-done.19.refs_1_
  11.0 2.2 %collective-permute-start.3 = (bf16[4,128,1024]{2,1,0:T(8,128)(2,1)S(1)}, bf16[4,128,1024]{2,1,0:T(8,128)(2,1)S(1)}, u32[]{:S(2)}, u32[]{:S(2)}) collective-permute-start(bf16[4,128,1024]{2,1,0:T(8,128)(2,1)S(1)} %get-tuple-element.64.refs_1_), channel_id=1, source_target_pairs={{0,2},{1,7},{2,4},{3,1},{4,6},{5,3},{6,0},{7,5},{8,10},{9,15},{10,... | collective-permute-start | bytes 3145736 | tf_op jit(solution)/shard_map/ppermute | solution.py:278
  13.1 0.0 collective-permute-done.20.refs_2_
  13.1 0.0 collective-permute-start.11
  13.1 18.9 %collective-permute-done.6.refs_3_ = bf16[4,128,1024]{2,1,0:T(8,128)(2,1)S(1)} collective-permute-done((bf16[4,128,1024]{2,1,0:T(8,128)(2,1)S(1)}, bf16[4,128,1024]{2,1,0:T(8,128)(2,1)S(1)}, u32[]{:S(2)}, u32[]{:S(2)}) %collective-permute-start.6) | collective-permute-done | bytes 1048608 | tf_op jit(solution)/shard_map/ppermute | solution.py:278
  32.0 3.4 %collective-permute-start = (bf16[4,128,1024]{2,1,0:T(8,128)(2,1)S(1)}, bf16[4,128,1024]{2,1,0:T(8,128)(2,1)S(1)}, u32[]{:S(2)}, u32[]{:S(2)}) collective-permute-start(bf16[4,128,1024]{2,1,0:T(8,128)(2,1)S(1)} %get-tuple-element.63.refs_2_), channel_id=1, source_target_pairs={{0,2},{1,7},{2,4},{3,1},{4,6},{5,3},{6,0},{7,5},{8,10},{9,15},{10,... | collective-permute-start | bytes 3145736 | tf_op jit(solution)/shard_map/ppermute | solution.py:278
  35.5 0.0 collective-permute-done.18.refs_0_
  35.5 0.0 collective-permute-start.9
  35.5 1.4 collective-permute-done.15.refs_1_
  36.8 0.4 collective-permute-start.17
  37.2 17.3 %collective-permute-done.3.refs_1_ = bf16[4,128,1024]{2,1,0:T(8,128)(2,1)S(1)} collective-permute-done((bf16[4,128,1024]{2,1,0:T(8,128)(2,1)S(1)}, bf16[4,128,1024]{2,1,0:T(8,128)(2,1)S(1)}, u32[]{:S(2)}, u32[]{:S(2)}) %collective-permute-start.3) | collective-permute-done | bytes 1048608 | tf_op jit(solution)/shard_map/ppermute | solution.py:278
  54.5 1.1 collective-permute-start.16
  55.6 3.7 %collective-permute-done.11.refs_1_ = bf16[4,128,1024]{2,1,0:T(8,128)(2,1)S(1)} collective-permute-done((bf16[4,128,1024]{2,1,0:T(8,128)(2,1)S(1)}, bf16[4,128,1024]{2,1,0:T(8,128)(2,1)S(1)}, u32[]{:S(2)}, u32[]{:S(2)}) %collective-permute-start.11) | collective-permute-done | bytes 1048608 | tf_op jit(solution)/shard_map/ppermute | solution.py:278
  59.3 0.2 collective-permute-start.14
  59.5 17.5 %collective-permute-done.refs_1_ = bf16[4,128,1024]{2,1,0:T(8,128)(2,1)S(1)} collective-permute-done((bf16[4,128,1024]{2,1,0:T(8,128)(2,1)S(1)}, bf16[4,128,1024]{2,1,0:T(8,128)(2,1)S(1)}, u32[]{:S(2)}, u32[]{:S(2)}) %collective-permute-start) | collective-permute-done | bytes 1048608 | tf_op jit(solution)/shard_map/ppermute | solution.py:278
  77.0 1.1 collective-permute-start.13
  78.0 1.5 collective-permute-done.9.refs_0_
  79.5 2.1 collective-permute-start.7
  81.7 0.0 collective-permute-done.17.refs_0_
  81.7 0.1 collective-permute-start.4
  81.8 0.0 collective-permute-done.16.refs_0_
  81.8 0.1 collective-permute-start.1
  81.9 0.0 collective-permute-done.14.refs_0_
  81.9 2.1 collective-permute-start.12
  84.0 0.0 collective-permute-done.13.refs_2_
  84.0 0.1 collective-permute-start.10
  84.1 9.5 %collective-permute-done.7.refs_1_ = bf16[4,128,1024]{2,1,0:T(8,128)(2,1)} collective-permute-done((bf16[4,128,1024]{2,1,0:T(8,128)(2,1)S(1)}, bf16[4,128,1024]{2,1,0:T(8,128)(2,1)}, u32[]{:S(2)}, u32[]{:S(2)}) %collective-permute-start.7) | collective-permute-done | bytes 1048608 | tf_op jit(solution)/shard_map/ppermute | solution.py:278
  93.6 1.9 collective-permute-start.8
  95.4 9.4 %collective-permute-done.4.refs_1_ = bf16[4,128,1024]{2,1,0:T(8,128)(2,1)} collective-permute-done((bf16[4,128,1024]{2,1,0:T(8,128)(2,1)S(1)}, bf16[4,128,1024]{2,1,0:T(8,128)(2,1)}, u32[]{:S(2)}, u32[]{:S(2)}) %collective-permute-start.4) | collective-permute-done | bytes 1048608 | tf_op jit(solution)/shard_map/ppermute | solution.py:278
  104.8 1.9 collective-permute-start.5
  106.7 9.4 %collective-permute-done.1.refs_0_ = bf16[4,128,1024]{2,1,0:T(8,128)(2,1)} collective-permute-done((bf16[4,128,1024]{2,1,0:T(8,128)(2,1)S(1)}, bf16[4,128,1024]{2,1,0:T(8,128)(2,1)}, u32[]{:S(2)}, u32[]{:S(2)}) %collective-permute-start.1) | collective-permute-done | bytes 1048608 | tf_op jit(solution)/shard_map/ppermute | solution.py:278
  116.1 1.9 collective-permute-start.2
  117.9 10.9 %shard_map.61 = (bf16[12,12,128,1024]{3,2,1,0:T(8,128)(2,1)}, bf16[12,12,128,1024]{3,2,1,0:T(8,128)(2,1)}, bf16[2,4,2,12,128,128]{5,4,3,2,1,0:T(8,128)(2,1)S(1)}...) custom-call(bf16[4,128,1024]{2,1,0:T(8,128)(2,1)S(1)} %shard_map.60.refs_0_, ...), custom_call_target="tpu_custom_call", output_to_operand_aliasing={{3}: (3, {}), {4}: (4, {})} | custom-call | flops 1572864 | bytes 1572864 | tf_op jit(solution)/shard_map/pallas_call | solution.py:224
  128.9 14.7 %shard_map.62 = (bf16[12,12,128,1024]{3,2,1,0:T(8,128)(2,1)}, bf16[12,12,128,1024]{3,2,1,0:T(8,128)(2,1)}, bf16[2,4,2,12,128,128]{5,4,3,2,1,0:T(8,128)(2,1)S(1)}...) custom-call(bf16[4,128,1024]{2,1,0:T(8,128)(2,1)S(1)} %collective-pe, ...), custom_call_target="tpu_custom_call", output_to_operand_aliasing={{3}: (4, {}), {4}: (5, {}), {0}: (6, {}), {1}: (7, {}), {2}... | custom-call | flops 2097152 | bytes 2097152 | tf_op jit(solution)/shard_map/pallas_call | solution.py:224
  143.5 7.4 %shard_map.63 = (bf16[12,12,128,1024]{3,2,1,0:T(8,128)(2,1)}, bf16[12,12,128,1024]{3,2,1,0:T(8,128)(2,1)}, bf16[2,4,2,12,128,128]{5,4,3,2,1,0:T(8,128)(2,1)S(1)}...) custom-call(bf16[4,128,1024]{2,1,0:T(8,128)(2,1)S(1)} %collective-pe, ...), custom_call_target="tpu_custom_call", output_to_operand_aliasing={{3}: (2, {}), {4}: (3, {}), {0}: (4, {}), {1}: (5, {}), {2}... | custom-call | flops 1048576 | bytes 1048576 | tf_op jit(solution)/shard_map/pallas_call | solution.py:224
  150.9 7.4 %shard_map.64 = (bf16[12,12,128,1024]{3,2,1,0:T(8,128)(2,1)}, bf16[12,12,128,1024]{3,2,1,0:T(8,128)(2,1)}, bf16[2,4,2,12,128,128]{5,4,3,2,1,0:T(8,128)(2,1)S(1)}...) custom-call(bf16[4,128,1024]{2,1,0:T(8,128)(2,1)S(1)} %collective-pe, ...), custom_call_target="tpu_custom_call", output_to_operand_aliasing={{3}: (2, {}), {4}: (3, {}), {0}: (4, {}), {1}: (5, {}), {2}... | custom-call | flops 1048576 | bytes 1048576 | tf_op jit(solution)/shard_map/pallas_call | solution.py:224
  158.4 7.6 %shard_map.65 = (bf16[12,12,128,1024]{3,2,1,0:T(8,128)(2,1)}, bf16[12,12,128,1024]{3,2,1,0:T(8,128)(2,1)}, bf16[2,4,2,12,128,128]{5,4,3,2,1,0:T(8,128)(2,1)S(1)}...) custom-call(bf16[4,128,1024]{2,1,0:T(8,128)(2,1)S(1)} %collective-pe, ...), custom_call_target="tpu_custom_call", output_to_operand_aliasing={{3}: (2, {}), {4}: (3, {}), {0}: (4, {}), {1}: (5, {}), {2}... | custom-call | flops 1048576 | bytes 1048576 | tf_op jit(solution)/shard_map/pallas_call | solution.py:224
  166.0 0.0 collective-permute-done.12.refs_0_
  166.0 11.0 %shard_map.66 = (bf16[12,12,128,1024]{3,2,1,0:T(8,128)(2,1)}, bf16[12,12,128,1024]{3,2,1,0:T(8,128)(2,1)}, bf16[2,4,2,12,128,128]{5,4,3,2,1,0:T(8,128)(2,1)S(1)}...) custom-call(bf16[4,128,1024]{2,1,0:T(8,128)(2,1)S(1)} %collective-pe, ...), custom_call_target="tpu_custom_call", output_to_operand_aliasing={{3}: (3, {}), {4}: (4, {}), {0}: (5, {}), {1}: (6, {}), {2}... | custom-call | flops 1572864 | bytes 1572864 | tf_op jit(solution)/shard_map/pallas_call | solution.py:224
  177.0 5.8 %shard_map.67 = (bf16[12,12,128,1024]{3,2,1,0:T(8,128)(2,1)}, bf16[12,12,128,1024]{3,2,1,0:T(8,128)(2,1)}, bf16[2,4,2,12,128,128]{5,4,3,2,1,0:T(8,128)(2,1)S(1)}...) custom-call(bf16[4,128,1024]{2,1,0:T(8,128)(2,1)} %collective-permut, ...), custom_call_target="tpu_custom_call", output_to_operand_aliasing={{3}: (1, {}), {4}: (2, {}), {0}: (3, {}), {1}: (4, {}), {2}... | custom-call | flops 524288 | bytes 524288 | tf_op jit(solution)/shard_map/pallas_call | solution.py:224
  182.8 0.0 collective-permute-done.10.refs_0_
  182.8 8.5 %shard_map.68 = (bf16[12,12,128,1024]{3,2,1,0:T(8,128)(2,1)}, bf16[12,12,128,1024]{3,2,1,0:T(8,128)(2,1)}, bf16[2,4,2,12,128,128]{5,4,3,2,1,0:T(8,128)(2,1)S(1)}...) custom-call(bf16[4,128,1024]{2,1,0:T(8,128)(2,1)} %collective-permut, ...), custom_call_target="tpu_custom_call", output_to_operand_aliasing={{3}: (2, {}), {4}: (3, {}), {0}: (4, {}), {1}: (5, {}), {2}... | custom-call | flops 1048576 | bytes 1048576 | tf_op jit(solution)/shard_map/pallas_call | solution.py:224
  191.3 0.0 collective-permute-done.8.refs_0_
  191.3 8.5 %shard_map.69 = (bf16[12,12,128,1024]{3,2,1,0:T(8,128)(2,1)}, bf16[12,12,128,1024]{3,2,1,0:T(8,128)(2,1)}, bf16[2,4,2,12,128,128]{5,4,3,2,1,0:T(8,128)(2,1)S(1)}...) custom-call(bf16[4,128,1024]{2,1,0:T(8,128)(2,1)} %collective-permut, ...), custom_call_target="tpu_custom_call", output_to_operand_aliasing={{3}: (2, {}), {4}: (3, {}), {0}: (4, {}), {1}: (5, {}), {2}... | custom-call | flops 1048576 | bytes 1048576 | tf_op jit(solution)/shard_map/pallas_call | solution.py:224
  199.8 0.0 collective-permute-done.5.refs_0_
  199.8 5.1 %shard_map.70 = (bf16[12,12,128,1024]{3,2,1,0:T(8,128)(2,1)}, bf16[12,12,128,1024]{3,2,1,0:T(8,128)(2,1)}, bf16[2,4,2,12,128,128]{5,4,3,2,1,0:T(8,128)(2,1)S(1)}...) custom-call(bf16[4,128,1024]{2,1,0:T(8,128)(2,1)} %collective-permut, ...), custom_call_target="tpu_custom_call", output_to_operand_aliasing={{3}: (1, {}), {4}: (2, {}), {0}: (3, {}), {1}: (4, {}), {2}... | custom-call | flops 524288 | bytes 524288 | tf_op jit(solution)/shard_map/pallas_call | solution.py:224
  205.0 5.7 %shard_map.71 = (bf16[12,12,128,1024]{3,2,1,0:T(8,128)(2,1)}, bf16[12,12,128,1024]{3,2,1,0:T(8,128)(2,1)}, bf16[2,4,2,12,128,128]{5,4,3,2,1,0:T(8,128)(2,1)S(1)}...) custom-call(bf16[4,128,1024]{2,1,0:T(8,128)(2,1)} %collective-permut, ...), custom_call_target="tpu_custom_call", output_to_operand_aliasing={{3}: (1, {}), {4}: (2, {}), {0}: (3, {}), {1}: (4, {}), {2}... | custom-call | flops 524288 | bytes 524288 | tf_op jit(solution)/shard_map/pallas_call | solution.py:224
  210.6 0.0 collective-permute-done.2.refs_0_
  210.6 6.2 %shard_map.72 = (bf16[12,12,128,1024]{3,2,1,0:T(8,128)(2,1)}, bf16[12,12,128,1024]{3,2,1,0:T(8,128)(2,1)}, bf16[2,4,2,12,128,128]{5,4,3,2,1,0:T(8,128)(2,1)S(1)}...) custom-call(bf16[4,128,1024]{2,1,0:T(8,128)(2,1)} %collective-permut, ...), custom_call_target="tpu_custom_call", output_to_operand_aliasing={{3}: (1, {}), {4}: (2, {}), {0}: (3, {}), {1}: (4, {}), {2}... | custom-call | flops 524288 | bytes 524288 | tf_op jit(solution)/shard_map/pallas_call | solution.py:224
Async XLA Ops:
  4.2 6.7 %collective-permute-start.19 = (bf16[4,128,1024]{2,1,0:T(8,128)(2,1)S(1)}, bf16[4,128,1024]{2,1,0:T(8,128)(2,1)S(1)}, u32[]{:S(2)}, u32[]{:S(2)}) collective-permute-start(bf16[4,128,1024]{2,1,0:T(8,128)(2,1)S(1)} %get-tuple-element.64.refs_1_), channel_id=1, source_target_pairs={{0,1},{1,0},{2,3},{3,2},{4,5},{5,4},{6,7},{7,6},{8,9},{9,8},{10,11... | collective-permute-start | bytes 3145736 | tf_op jit(solution)/shard_map/ppermute | solution.py:278
  5.0 8.1 %collective-permute-start.20 = (bf16[4,128,1024]{2,1,0:T(8,128)(2,1)S(1)}, bf16[4,128,1024]{2,1,0:T(8,128)(2,1)S(1)}, u32[]{:S(2)}, u32[]{:S(2)}) collective-permute-start(bf16[4,128,1024]{2,1,0:T(8,128)(2,1)S(1)} %get-tuple-element.63.refs_2_), channel_id=1, source_target_pairs={{0,1},{1,0},{2,3},{3,2},{4,5},{5,4},{6,7},{7,6},{8,9},{9,8},{10,11... | collective-permute-start | bytes 3145736 | tf_op jit(solution)/shard_map/ppermute | solution.py:278
  6.8 25.3 %collective-permute-start.6 = (bf16[4,128,1024]{2,1,0:T(8,128)(2,1)S(1)}, bf16[4,128,1024]{2,1,0:T(8,128)(2,1)S(1)}, u32[]{:S(2)}, u32[]{:S(2)}) collective-permute-start(bf16[4,128,1024]{2,1,0:T(8,128)(2,1)S(1)} %shard_map.60.refs_0_), channel_id=1, source_target_pairs={{0,2},{1,7},{2,4},{3,1},{4,6},{5,3},{6,0},{7,5},{8,10},{9,15},{10,... | collective-permute-start | bytes 3145736 | tf_op jit(solution)/shard_map/ppermute | solution.py:278
  10.5 25.0 %collective-permute-start.18 = (bf16[4,128,1024]{2,1,0:T(8,128)(2,1)S(1)}, bf16[4,128,1024]{2,1,0:T(8,128)(2,1)S(1)}, u32[]{:S(2)}, u32[]{:S(2)}) collective-permute-start(bf16[4,128,1024]{2,1,0:T(8,128)(2,1)S(1)} %shard_map.60.refs_0_), channel_id=1, source_target_pairs={{0,1},{1,0},{2,3},{3,2},{4,5},{5,4},{6,7},{7,6},{8,9},{9,8},{10,11... | collective-permute-start | bytes 3145736 | tf_op jit(solution)/shard_map/ppermute | solution.py:278
  10.5 26.4 %collective-permute-start.15 = (bf16[4,128,1024]{2,1,0:T(8,128)(2,1)S(1)}, bf16[4,128,1024]{2,1,0:T(8,128)(2,1)S(1)}, u32[]{:S(2)}, u32[]{:S(2)}) collective-permute-start(bf16[4,128,1024]{2,1,0:T(8,128)(2,1)S(1)} %shard_map.60.refs_0_), channel_id=1, source_target_pairs={{0,6},{1,3},{2,0},{3,5},{4,2},{5,7},{6,4},{7,1},{8,14},{9,11},{10,... | collective-permute-start | bytes 3145736 | tf_op jit(solution)/shard_map/ppermute | solution.py:278
  11.0 43.6 %collective-permute-start.3 = (bf16[4,128,1024]{2,1,0:T(8,128)(2,1)S(1)}, bf16[4,128,1024]{2,1,0:T(8,128)(2,1)S(1)}, u32[]{:S(2)}, u32[]{:S(2)}) collective-permute-start(bf16[4,128,1024]{2,1,0:T(8,128)(2,1)S(1)} %get-tuple-element.64.refs_1_), channel_id=1, source_target_pairs={{0,2},{1,7},{2,4},{3,1},{4,6},{5,3},{6,0},{7,5},{8,10},{9,15},{10,... | collective-permute-start | bytes 3145736 | tf_op jit(solution)/shard_map/ppermute | solution.py:278
  13.1 46.2 %collective-permute-start.11 = (bf16[4,128,1024]{2,1,0:T(8,128)(2,1)S(1)}, bf16[4,128,1024]{2,1,0:T(8,128)(2,1)S(1)}, u32[]{:S(2)}, u32[]{:S(2)}) collective-permute-start(bf16[4,128,1024]{2,1,0:T(8,128)(2,1)S(1)} %get-tuple-element.64.refs_1_), channel_id=1, source_target_pairs={{0,6},{1,3},{2,0},{3,5},{4,2},{5,7},{6,4},{7,1},{8,14},{9,11},{10,... | collective-permute-start | bytes 3145736 | tf_op jit(solution)/shard_map/ppermute | solution.py:278
  32.0 44.9 %collective-permute-start = (bf16[4,128,1024]{2,1,0:T(8,128)(2,1)S(1)}, bf16[4,128,1024]{2,1,0:T(8,128)(2,1)S(1)}, u32[]{:S(2)}, u32[]{:S(2)}) collective-permute-start(bf16[4,128,1024]{2,1,0:T(8,128)(2,1)S(1)} %get-tuple-element.63.refs_2_), channel_id=1, source_target_pairs={{0,2},{1,7},{2,4},{3,1},{4,6},{5,3},{6,0},{7,5},{8,10},{9,15},{10,... | collective-permute-start | bytes 3145736 | tf_op jit(solution)/shard_map/ppermute | solution.py:278
  35.5 44.1 %collective-permute-start.9 = (bf16[4,128,1024]{2,1,0:T(8,128)(2,1)S(1)}, bf16[4,128,1024]{2,1,0:T(8,128)(2,1)}, u32[]{:S(2)}, u32[]{:S(2)}) collective-permute-start(bf16[4,128,1024]{2,1,0:T(8,128)(2,1)S(1)} %get-tuple-element.63.refs_2_), channel_id=1, source_target_pairs={{0,6},{1,3},{2,0},{3,5},{4,2},{5,7},{6,4},{7,1},{8,14},{9,11},{10,... | collective-permute-start | bytes 3145736 | tf_op jit(solution)/shard_map/ppermute | solution.py:278
  36.8 44.8 %collective-permute-start.17 = (bf16[4,128,1024]{2,1,0:T(8,128)(2,1)S(1)}, bf16[4,128,1024]{2,1,0:T(8,128)(2,1)S(1)}, u32[]{:S(2)}, u32[]{:S(2)}) collective-permute-start(bf16[4,128,1024]{2,1,0:T(8,128)(2,1)S(1)} %collective-permute-done.6.refs_3_), channel_id=1, source_target_pairs={{0,1},{1,0},{2,3},{3,2},{4,5},{5,4},{6,7},{7,6},{8,9},{9,8},{10,11... | collective-permute-start | bytes 3145736 | tf_op jit(solution)/shard_map/ppermute | solution.py:278
  54.5 27.2 %collective-permute-start.16 = (bf16[4,128,1024]{2,1,0:T(8,128)(2,1)S(1)}, bf16[4,128,1024]{2,1,0:T(8,128)(2,1)S(1)}, u32[]{:S(2)}, u32[]{:S(2)}) collective-permute-start(bf16[4,128,1024]{2,1,0:T(8,128)(2,1)S(1)} %collective-permute-done.15.refs_1_), channel_id=1, source_target_pairs={{0,1},{1,0},{2,3},{3,2},{4,5},{5,4},{6,7},{7,6},{8,9},{9,8},{10,11... | collective-permute-start | bytes 3145736 | tf_op jit(solution)/shard_map/ppermute | solution.py:278
  59.3 22.6 %collective-permute-start.14 = (bf16[4,128,1024]{2,1,0:T(8,128)(2,1)S(1)}, bf16[4,128,1024]{2,1,0:T(8,128)(2,1)S(1)}, u32[]{:S(2)}, u32[]{:S(2)}) collective-permute-start(bf16[4,128,1024]{2,1,0:T(8,128)(2,1)S(1)} %collective-permute-done.3.refs_1_), channel_id=1, source_target_pairs={{0,1},{1,0},{2,3},{3,2},{4,5},{5,4},{6,7},{7,6},{8,9},{9,8},{10,11... | collective-permute-start | bytes 3145736 | tf_op jit(solution)/shard_map/ppermute | solution.py:278
  77.0 7.0 %collective-permute-start.13 = (bf16[4,128,1024]{2,1,0:T(8,128)(2,1)S(1)}, bf16[4,128,1024]{2,1,0:T(8,128)(2,1)S(1)}, u32[]{:S(2)}, u32[]{:S(2)}) collective-permute-start(bf16[4,128,1024]{2,1,0:T(8,128)(2,1)S(1)} %collective-permute-done.refs_1_), channel_id=1, source_target_pairs={{0,1},{1,0},{2,3},{3,2},{4,5},{5,4},{6,7},{7,6},{8,9},{9,8},{10,11... | collective-permute-start | bytes 3145736 | tf_op jit(solution)/shard_map/ppermute | solution.py:278
  79.5 14.0 %collective-permute-start.7 = (bf16[4,128,1024]{2,1,0:T(8,128)(2,1)S(1)}, bf16[4,128,1024]{2,1,0:T(8,128)(2,1)}, u32[]{:S(2)}, u32[]{:S(2)}) collective-permute-start(bf16[4,128,1024]{2,1,0:T(8,128)(2,1)S(1)} %collective-permute-done.6.refs_3_), channel_id=1, source_target_pairs={{0,2},{1,7},{2,4},{3,1},{4,6},{5,3},{6,0},{7,5},{8,10},{9,15},{10,... | collective-permute-start | bytes 3145736 | tf_op jit(solution)/shard_map/ppermute | solution.py:278
  81.7 23.1 %collective-permute-start.4 = (bf16[4,128,1024]{2,1,0:T(8,128)(2,1)S(1)}, bf16[4,128,1024]{2,1,0:T(8,128)(2,1)}, u32[]{:S(2)}, u32[]{:S(2)}) collective-permute-start(bf16[4,128,1024]{2,1,0:T(8,128)(2,1)S(1)} %collective-permute-done.3.refs_1_), channel_id=1, source_target_pairs={{0,2},{1,7},{2,4},{3,1},{4,6},{5,3},{6,0},{7,5},{8,10},{9,15},{10,... | collective-permute-start | bytes 3145736 | tf_op jit(solution)/shard_map/ppermute | solution.py:278
  81.8 34.3 %collective-permute-start.1 = (bf16[4,128,1024]{2,1,0:T(8,128)(2,1)S(1)}, bf16[4,128,1024]{2,1,0:T(8,128)(2,1)}, u32[]{:S(2)}, u32[]{:S(2)}) collective-permute-start(bf16[4,128,1024]{2,1,0:T(8,128)(2,1)S(1)} %collective-permute-done.refs_1_), channel_id=1, source_target_pairs={{0,2},{1,7},{2,4},{3,1},{4,6},{5,3},{6,0},{7,5},{8,10},{9,15},{10,... | collective-permute-start | bytes 3145736 | tf_op jit(solution)/shard_map/ppermute | solution.py:278
  81.9 84.1 %collective-permute-start.12 = (bf16[4,128,1024]{2,1,0:T(8,128)(2,1)S(1)}, bf16[4,128,1024]{2,1,0:T(8,128)(2,1)S(1)}, u32[]{:S(2)}, u32[]{:S(2)}) collective-permute-start(bf16[4,128,1024]{2,1,0:T(8,128)(2,1)S(1)} %collective-permute-done.11.refs_1_), channel_id=1, source_target_pairs={{0,1},{1,0},{2,3},{3,2},{4,5},{5,4},{6,7},{7,6},{8,9},{9,8},{10,11... | collective-permute-start | bytes 3145736 | tf_op jit(solution)/shard_map/ppermute | solution.py:278
  84.0 98.8 %collective-permute-start.10 = (bf16[4,128,1024]{2,1,0:T(8,128)(2,1)}, bf16[4,128,1024]{2,1,0:T(8,128)(2,1)}, u32[]{:S(2)}, u32[]{:S(2)}) collective-permute-start(bf16[4,128,1024]{2,1,0:T(8,128)(2,1)} %collective-permute-done.9.refs_0_), channel_id=1, source_target_pairs={{0,1},{1,0},{2,3},{3,2},{4,5},{5,4},{6,7},{7,6},{8,9},{9,8},{10,11... | collective-permute-start | bytes 3145736 | tf_op jit(solution)/shard_map/ppermute | solution.py:278
  93.6 97.8 %collective-permute-start.8 = (bf16[4,128,1024]{2,1,0:T(8,128)(2,1)}, bf16[4,128,1024]{2,1,0:T(8,128)(2,1)}, u32[]{:S(2)}, u32[]{:S(2)}) collective-permute-start(bf16[4,128,1024]{2,1,0:T(8,128)(2,1)} %collective-permute-done.7.refs_1_), channel_id=1, source_target_pairs={{0,1},{1,0},{2,3},{3,2},{4,5},{5,4},{6,7},{7,6},{8,9},{9,8},{10,11... | collective-permute-start | bytes 3145736 | tf_op jit(solution)/shard_map/ppermute | solution.py:278
  104.8 95.0 %collective-permute-start.5 = (bf16[4,128,1024]{2,1,0:T(8,128)(2,1)}, bf16[4,128,1024]{2,1,0:T(8,128)(2,1)}, u32[]{:S(2)}, u32[]{:S(2)}) collective-permute-start(bf16[4,128,1024]{2,1,0:T(8,128)(2,1)} %collective-permute-done.4.refs_1_), channel_id=1, source_target_pairs={{0,1},{1,0},{2,3},{3,2},{4,5},{5,4},{6,7},{7,6},{8,9},{9,8},{10,11... | collective-permute-start | bytes 3145736 | tf_op jit(solution)/shard_map/ppermute | solution.py:278
  116.1 94.6 %collective-permute-start.2 = (bf16[4,128,1024]{2,1,0:T(8,128)(2,1)}, bf16[4,128,1024]{2,1,0:T(8,128)(2,1)}, u32[]{:S(2)}, u32[]{:S(2)}) collective-permute-start(bf16[4,128,1024]{2,1,0:T(8,128)(2,1)} %collective-permute-done.1.refs_0_), channel_id=1, source_target_pairs={{0,1},{1,0},{2,3},{3,2},{4,5},{5,4},{6,7},{7,6},{8,9},{9,8},{10,11... | collective-permute-start | bytes 3145736 | tf_op jit(solution)/shard_map/ppermute | solution.py:278

commit v3 on v2

--- a/solution.py
+++ b/solution.py
@@ -104,7 +104,7 @@
 def project_kernel(pieces, group, slot0, before, last, *refs):
     n_x = len(pieces)
     x_refs, (wk_ref, wv_ref) = refs[:n_x], refs[n_x:n_x + 2]
-    k_ref, v_ref, o_buf, _, _, x_buf, x_sem, o_sem = refs[-8:]
+    k_ref, v_ref, o_buf, _, wv_held, x_buf, x_sem, o_sem, w_sem = refs[-9:]
     layers, heads = k_ref.shape[0], k_ref.shape[2]
     tokens, depth = x_refs[0].shape[1:]
     me = lax.axis_index("tp")
@@ -116,6 +116,10 @@
     def x_copy(p):
         return pltpu.make_async_copy(x_refs[p], x_buf.at[pl.ds(starts[p], pieces[p][0])], x_sem.at[p])
 
+    load = None if before else pltpu.make_async_copy(wv_ref, wv_held, w_sem)
+    if load:
+        load.start()
+        wv_ref = wv_held
     for p in far:
         x_copy(p).start()
 
@@ -179,6 +183,10 @@
         x = x.reshape(group * tokens, depth)
         chunk = 4
         for w, w_ref in enumerate((wk_ref, wv_ref)):
+            if w and load:
+                @pl.when(s == 0)
+                def _():
+                    load.wait()
             for layer in range(0, layers, chunk):
                 rows = w_ref[layer * heads:(layer + chunk) * heads, :]
                 acc = lax.dot_general(rows, x, (((1,), (1,)), ((), ())), preferred_element_type=jnp.float32)
@@ -217,17 +225,19 @@
     old, weights = state[:-2], state[-2:]
     operands = [*arrays, *weights, *old]
     n_x = len(arrays)
-    aliases = {n_x: 3, n_x + 1: 4}
+    aliases = {n_x: 3}
     if old:
-        aliases.update({n_x + 2 + i: i for i in range(3)})
+        aliases.update({n_x + 1: 4, **{n_x + 2 + i: i for i in range(3)}})
+    else:
+        operands[-1] = pltpu.with_memory_space_constraint(operands[-1], pltpu.HBM)
     staged = total if n_x > 1 or layout[0][3] else 1
     state = pl.pallas_call(
         functools.partial(project_kernel, layout, group, slot0, before, last),
-        in_specs=[ANY if far else VMEM for _, _, _, far in layout] + [VMEM] * 2 + [ANY, ANY, VMEM][:len(old)],
+        in_specs=[ANY if far else VMEM for _, _, _, far in layout] + [VMEM, VMEM if old else HBM] + [ANY, ANY, VMEM][:len(old)],
         out_specs=[ANY, ANY, VMEM, VMEM, VMEM],
         out_shape=[cache, cache, hold, *(jax.ShapeDtypeStruct(w.shape, w.dtype) for w in weights)],
         input_output_aliases=aliases,
-        scratch_shapes=[pltpu.VMEM((staged, tokens, depth), jnp.bfloat16), pltpu.SemaphoreType.DMA((n_x,)), pltpu.SemaphoreType.DMA((2, 4, 2))],
+        scratch_shapes=[pltpu.VMEM((staged, tokens, depth), jnp.bfloat16), pltpu.SemaphoreType.DMA((n_x,)), pltpu.SemaphoreType.DMA((2, 4, 2)), pltpu.SemaphoreType.DMA],
         compiler_params=pltpu.CompilerParams(vmem_limit_bytes=6 * MIB),
         cost_estimate=pl.CostEstimate(flops=total * tokens * depth, bytes_accessed=total * tokens * depth, transcendentals=0),
     )(*operands)
@@ -263,10 +273,10 @@
             if op in ("n0", "n1"):
                 done = int(op[-1])
                 counts = sizes[1:] if done else sizes[:1]
-                made = norm_pieces(enc_out, norm_scale, firsts[done], counts, (wk, wv) if done else ())
+                made = norm_pieces(enc_out, norm_scale, firsts[done], counts, (wk,) if done else ())
                 if done:
-                    *made, w_key, w_value = made
-                    weights = (w_key, w_value)
+                    *made, w_key = made
+                    weights = (w_key, wv)
                 for part, x in enumerate(made, done):
                     pieces[f"p{part}"] = (x, firsts[part], home, False)
             elif isinstance(op, tuple):

time: 217 us -> 217 us (level)
  transfers between devices with their start and end apart: 21 -> 21, of which waited for: 9 -> 9; matrix products, arithmetic and copies ran while one was open for 0% -> 0% of each run, Pallas kernels for 43% -> 44%
where the time goes in v3:
time: 217 us
  Pallas kernels  104 us (48%)
  waiting for transfers between devices  88.6 us (41%)
  starting transfers between devices  23.4 us (11%)
    pallas_call x12, Pallas kernels, project(): pl.pallas_call(functools.partial(project_kernel, layout, group, slot0, be...  99.4 us
    ppermute x21, waiting for transfers between devices, body(): x = lax.ppermute(x, 'tp', perms[way])  88.6 us
    ppermute x21, starting transfers between devices, body(): x = lax.ppermute(x, 'tp', perms[way])  23.4 us
  transfers between devices with their start and end apart: 21, of which 9 were waited for; matrix products, arithmetic and copies ran while one was open for 0% of the time, Pallas kernels for 44%

profile of v3, /device:TPU:113, one launch (start us, length us, event | category | flops | bytes accessed | tf_op | source)
XLA Modules:
  0.0 216.7 jit_solution(11124966717086155035)
XLA Ops:
  0.6 2.7 %shard_map.59 = (bf16[4,128,1024]{2,1,0:T(8,128)(2,1)S(1)}, bf16[4,128,1024]{2,1,0:T(8,128)(2,1)S(1)}, bf16[1536,1024]{1,0:T(8,128)(2,1)S(1)}) custom-call(bf16[12,128,1024]{2,1,0:T(8,128)(2,1)} %x_ref.3, bf16[1024]{0:T(1024)(128)(2,1)} %scale_ref.3, bf16[1536,1024]{1,0:T(8,128)(2,1)} %bitcast.14), custom_call_target="tpu_custom_call" | custom-call | flops 8388608 | bytes 4194304 | tf_op jit(solution)/shard_map/pallas_call | solution.py:93
  3.3 0.8 collective-permute-start.19
  4.1 0.1 collective-permute-start.20
  4.2 1.6 shard_map.60.refs_0_
  5.8 3.7 %collective-permute-start.6 = (bf16[4,128,1024]{2,1,0:T(8,128)(2,1)S(1)}, bf16[4,128,1024]{2,1,0:T(8,128)(2,1)S(1)}, u32[]{:S(2)}, u32[]{:S(2)}) collective-permute-start(bf16[4,128,1024]{2,1,0:T(8,128)(2,1)S(1)} %shard_map.60.refs_0_), channel_id=1, source_target_pairs={{0,2},{1,7},{2,4},{3,1},{4,6},{5,3},{6,0},{7,5},{8,10},{9,15},{10,... | collective-permute-start | bytes 3145736 | tf_op jit(solution)/shard_map/ppermute | solution.py:288
  9.5 0.0 collective-permute-start.18
  9.5 0.5 collective-permute-start.15
  10.0 0.0 collective-permute-done.19.refs_1_
  10.0 2.2 %collective-permute-start.3 = (bf16[4,128,1024]{2,1,0:T(8,128)(2,1)S(1)}, bf16[4,128,1024]{2,1,0:T(8,128)(2,1)S(1)}, u32[]{:S(2)}, u32[]{:S(2)}) collective-permute-start(bf16[4,128,1024]{2,1,0:T(8,128)(2,1)S(1)} %get-tuple-element.63.refs_1_), channel_id=1, source_target_pairs={{0,2},{1,7},{2,4},{3,1},{4,6},{5,3},{6,0},{7,5},{8,10},{9,15},{10,... | collective-permute-start | bytes 3145736 | tf_op jit(solution)/shard_map/ppermute | solution.py:288
  12.2 0.0 collective-permute-done.20.refs_2_
  12.2 0.0 collective-permute-start.11
  12.2 18.9 %collective-permute-done.6.refs_3_ = bf16[4,128,1024]{2,1,0:T(8,128)(2,1)S(1)} collective-permute-done((bf16[4,128,1024]{2,1,0:T(8,128)(2,1)S(1)}, bf16[4,128,1024]{2,1,0:T(8,128)(2,1)S(1)}, u32[]{:S(2)}, u32[]{:S(2)}) %collective-permute-start.6) | collective-permute-done | bytes 1048608 | tf_op jit(solution)/shard_map/ppermute | solution.py:288
  31.1 3.4 %collective-permute-start = (bf16[4,128,1024]{2,1,0:T(8,128)(2,1)S(1)}, bf16[4,128,1024]{2,1,0:T(8,128)(2,1)S(1)}, u32[]{:S(2)}, u32[]{:S(2)}) collective-permute-start(bf16[4,128,1024]{2,1,0:T(8,128)(2,1)S(1)} %get-tuple-element.62.refs_2_), channel_id=1, source_target_pairs={{0,2},{1,7},{2,4},{3,1},{4,6},{5,3},{6,0},{7,5},{8,10},{9,15},{10,... | collective-permute-start | bytes 3145736 | tf_op jit(solution)/shard_map/ppermute | solution.py:288
  34.5 0.0 collective-permute-done.18.refs_0_
  34.5 0.0 collective-permute-start.9
  34.5 1.4 collective-permute-done.15.refs_1_
  35.9 0.4 collective-permute-start.17
  36.2 17.3 %collective-permute-done.3.refs_1_ = bf16[4,128,1024]{2,1,0:T(8,128)(2,1)S(1)} collective-permute-done((bf16[4,128,1024]{2,1,0:T(8,128)(2,1)S(1)}, bf16[4,128,1024]{2,1,0:T(8,128)(2,1)S(1)}, u32[]{:S(2)}, u32[]{:S(2)}) %collective-permute-start.3) | collective-permute-done | bytes 1048608 | tf_op jit(solution)/shard_map/ppermute | solution.py:288
  53.6 1.1 collective-permute-start.16
  54.6 3.7 %collective-permute-done.11.refs_1_ = bf16[4,128,1024]{2,1,0:T(8,128)(2,1)S(1)} collective-permute-done((bf16[4,128,1024]{2,1,0:T(8,128)(2,1)S(1)}, bf16[4,128,1024]{2,1,0:T(8,128)(2,1)S(1)}, u32[]{:S(2)}, u32[]{:S(2)}) %collective-permute-start.11) | collective-permute-done | bytes 1048608 | tf_op jit(solution)/shard_map/ppermute | solution.py:288
  58.4 0.2 collective-permute-start.14
  58.5 17.5 %collective-permute-done.refs_1_ = bf16[4,128,1024]{2,1,0:T(8,128)(2,1)S(1)} collective-permute-done((bf16[4,128,1024]{2,1,0:T(8,128)(2,1)S(1)}, bf16[4,128,1024]{2,1,0:T(8,128)(2,1)S(1)}, u32[]{:S(2)}, u32[]{:S(2)}) %collective-permute-start) | collective-permute-done | bytes 1048608 | tf_op jit(solution)/shard_map/ppermute | solution.py:288
  76.0 1.1 collective-permute-start.13
  77.1 1.5 collective-permute-done.9.refs_0_
  78.6 2.1 collective-permute-start.7
  80.7 0.0 collective-permute-done.17.refs_0_
  80.7 0.1 collective-permute-start.4
  80.8 0.0 collective-permute-done.16.refs_0_
  80.8 0.1 collective-permute-start.1
  80.9 0.0 collective-permute-done.14.refs_0_
  80.9 2.1 collective-permute-start.12
  83.0 0.0 collective-permute-done.13.refs_2_
  83.1 0.1 collective-permute-start.10
  83.1 9.5 %collective-permute-done.7.refs_1_ = bf16[4,128,1024]{2,1,0:T(8,128)(2,1)} collective-permute-done((bf16[4,128,1024]{2,1,0:T(8,128)(2,1)S(1)}, bf16[4,128,1024]{2,1,0:T(8,128)(2,1)}, u32[]{:S(2)}, u32[]{:S(2)}) %collective-permute-start.7) | collective-permute-done | bytes 1048608 | tf_op jit(solution)/shard_map/ppermute | solution.py:288
  92.6 1.9 collective-permute-start.8
  94.5 9.4 %collective-permute-done.4.refs_1_ = bf16[4,128,1024]{2,1,0:T(8,128)(2,1)} collective-permute-done((bf16[4,128,1024]{2,1,0:T(8,128)(2,1)S(1)}, bf16[4,128,1024]{2,1,0:T(8,128)(2,1)}, u32[]{:S(2)}, u32[]{:S(2)}) %collective-permute-start.4) | collective-permute-done | bytes 1048608 | tf_op jit(solution)/shard_map/ppermute | solution.py:288
  103.9 1.9 collective-permute-start.5
  105.7 9.4 %collective-permute-done.1.refs_0_ = bf16[4,128,1024]{2,1,0:T(8,128)(2,1)} collective-permute-done((bf16[4,128,1024]{2,1,0:T(8,128)(2,1)S(1)}, bf16[4,128,1024]{2,1,0:T(8,128)(2,1)}, u32[]{:S(2)}, u32[]{:S(2)}) %collective-permute-start.1) | collective-permute-done | bytes 1048608 | tf_op jit(solution)/shard_map/ppermute | solution.py:288
  115.1 1.9 collective-permute-start.2
  117.0 11.5 %shard_map.61 = (bf16[12,12,128,1024]{3,2,1,0:T(8,128)(2,1)}, bf16[12,12,128,1024]{3,2,1,0:T(8,128)(2,1)}, bf16[2,4,2,12,128,128]{5,4,3,2,1,0:T(8,128)(2,1)S(1)}...) custom-call(bf16[4,128,1024]{2,1,0:T(8,128)(2,1)S(1)} %shard_map.60.refs_0_, ...), custom_call_target="tpu_custom_call", output_to_operand_aliasing={{3}: (3, {})} | custom-call | flops 1572864 | bytes 1572864 | tf_op jit(solution)/shard_map/pallas_call | solution.py:234
  128.5 14.7 %shard_map.62 = (bf16[12,12,128,1024]{3,2,1,0:T(8,128)(2,1)}, bf16[12,12,128,1024]{3,2,1,0:T(8,128)(2,1)}, bf16[2,4,2,12,128,128]{5,4,3,2,1,0:T(8,128)(2,1)S(1)}...) custom-call(bf16[4,128,1024]{2,1,0:T(8,128)(2,1)S(1)} %collective-pe, ...), custom_call_target="tpu_custom_call", output_to_operand_aliasing={{3}: (4, {}), {4}: (5, {}), {0}: (6, {}), {1}: (7, {}), {2}... | custom-call | flops 2097152 | bytes 2097152 | tf_op jit(solution)/shard_map/pallas_call | solution.py:234
  143.2 7.4 %shard_map.63 = (bf16[12,12,128,1024]{3,2,1,0:T(8,128)(2,1)}, bf16[12,12,128,1024]{3,2,1,0:T(8,128)(2,1)}, bf16[2,4,2,12,128,128]{5,4,3,2,1,0:T(8,128)(2,1)S(1)}...) custom-call(bf16[4,128,1024]{2,1,0:T(8,128)(2,1)S(1)} %collective-pe, ...), custom_call_target="tpu_custom_call", output_to_operand_aliasing={{3}: (2, {}), {4}: (3, {}), {0}: (4, {}), {1}: (5, {}), {2}... | custom-call | flops 1048576 | bytes 1048576 | tf_op jit(solution)/shard_map/pallas_call | solution.py:234
  150.6 7.4 %shard_map.64 = (bf16[12,12,128,1024]{3,2,1,0:T(8,128)(2,1)}, bf16[12,12,128,1024]{3,2,1,0:T(8,128)(2,1)}, bf16[2,4,2,12,128,128]{5,4,3,2,1,0:T(8,128)(2,1)S(1)}...) custom-call(bf16[4,128,1024]{2,1,0:T(8,128)(2,1)S(1)} %collective-pe, ...), custom_call_target="tpu_custom_call", output_to_operand_aliasing={{3}: (2, {}), {4}: (3, {}), {0}: (4, {}), {1}: (5, {}), {2}... | custom-call | flops 1048576 | bytes 1048576 | tf_op jit(solution)/shard_map/pallas_call | solution.py:234
  158.0 7.6 %shard_map.65 = (bf16[12,12,128,1024]{3,2,1,0:T(8,128)(2,1)}, bf16[12,12,128,1024]{3,2,1,0:T(8,128)(2,1)}, bf16[2,4,2,12,128,128]{5,4,3,2,1,0:T(8,128)(2,1)S(1)}...) custom-call(bf16[4,128,1024]{2,1,0:T(8,128)(2,1)S(1)} %collective-pe, ...), custom_call_target="tpu_custom_call", output_to_operand_aliasing={{3}: (2, {}), {4}: (3, {}), {0}: (4, {}), {1}: (5, {}), {2}... | custom-call | flops 1048576 | bytes 1048576 | tf_op jit(solution)/shard_map/pallas_call | solution.py:234
  165.7 0.0 collective-permute-done.12.refs_0_
  165.7 11.1 %shard_map.66 = (bf16[12,12,128,1024]{3,2,1,0:T(8,128)(2,1)}, bf16[12,12,128,1024]{3,2,1,0:T(8,128)(2,1)}, bf16[2,4,2,12,128,128]{5,4,3,2,1,0:T(8,128)(2,1)S(1)}...) custom-call(bf16[4,128,1024]{2,1,0:T(8,128)(2,1)S(1)} %collective-pe, ...), custom_call_target="tpu_custom_call", output_to_operand_aliasing={{3}: (3, {}), {4}: (4, {}), {0}: (5, {}), {1}: (6, {}), {2}... | custom-call | flops 1572864 | bytes 1572864 | tf_op jit(solution)/shard_map/pallas_call | solution.py:234
  176.7 5.8 %shard_map.67 = (bf16[12,12,128,1024]{3,2,1,0:T(8,128)(2,1)}, bf16[12,12,128,1024]{3,2,1,0:T(8,128)(2,1)}, bf16[2,4,2,12,128,128]{5,4,3,2,1,0:T(8,128)(2,1)S(1)}...) custom-call(bf16[4,128,1024]{2,1,0:T(8,128)(2,1)} %collective-permut, ...), custom_call_target="tpu_custom_call", output_to_operand_aliasing={{3}: (1, {}), {4}: (2, {}), {0}: (3, {}), {1}: (4, {}), {2}... | custom-call | flops 524288 | bytes 524288 | tf_op jit(solution)/shard_map/pallas_call | solution.py:234
  182.5 0.0 collective-permute-done.10.refs_0_
  182.5 8.5 %shard_map.68 = (bf16[12,12,128,1024]{3,2,1,0:T(8,128)(2,1)}, bf16[12,12,128,1024]{3,2,1,0:T(8,128)(2,1)}, bf16[2,4,2,12,128,128]{5,4,3,2,1,0:T(8,128)(2,1)S(1)}...) custom-call(bf16[4,128,1024]{2,1,0:T(8,128)(2,1)} %collective-permut, ...), custom_call_target="tpu_custom_call", output_to_operand_aliasing={{3}: (2, {}), {4}: (3, {}), {0}: (4, {}), {1}: (5, {}), {2}... | custom-call | flops 1048576 | bytes 1048576 | tf_op jit(solution)/shard_map/pallas_call | solution.py:234
  191.0 0.0 collective-permute-done.8.refs_0_
  191.0 8.5 %shard_map.69 = (bf16[12,12,128,1024]{3,2,1,0:T(8,128)(2,1)}, bf16[12,12,128,1024]{3,2,1,0:T(8,128)(2,1)}, bf16[2,4,2,12,128,128]{5,4,3,2,1,0:T(8,128)(2,1)S(1)}...) custom-call(bf16[4,128,1024]{2,1,0:T(8,128)(2,1)} %collective-permut, ...), custom_call_target="tpu_custom_call", output_to_operand_aliasing={{3}: (2, {}), {4}: (3, {}), {0}: (4, {}), {1}: (5, {}), {2}... | custom-call | flops 1048576 | bytes 1048576 | tf_op jit(solution)/shard_map/pallas_call | solution.py:234
  199.5 0.0 collective-permute-done.5.refs_0_
  199.6 5.1 %shard_map.70 = (bf16[12,12,128,1024]{3,2,1,0:T(8,128)(2,1)}, bf16[12,12,128,1024]{3,2,1,0:T(8,128)(2,1)}, bf16[2,4,2,12,128,128]{5,4,3,2,1,0:T(8,128)(2,1)S(1)}...) custom-call(bf16[4,128,1024]{2,1,0:T(8,128)(2,1)} %collective-permut, ...), custom_call_target="tpu_custom_call", output_to_operand_aliasing={{3}: (1, {}), {4}: (2, {}), {0}: (3, {}), {1}: (4, {}), {2}... | custom-call | flops 524288 | bytes 524288 | tf_op jit(solution)/shard_map/pallas_call | solution.py:234
  204.7 5.7 %shard_map.71 = (bf16[12,12,128,1024]{3,2,1,0:T(8,128)(2,1)}, bf16[12,12,128,1024]{3,2,1,0:T(8,128)(2,1)}, bf16[2,4,2,12,128,128]{5,4,3,2,1,0:T(8,128)(2,1)S(1)}...) custom-call(bf16[4,128,1024]{2,1,0:T(8,128)(2,1)} %collective-permut, ...), custom_call_target="tpu_custom_call", output_to_operand_aliasing={{3}: (1, {}), {4}: (2, {}), {0}: (3, {}), {1}: (4, {}), {2}... | custom-call | flops 524288 | bytes 524288 | tf_op jit(solution)/shard_map/pallas_call | solution.py:234
  210.3 0.0 collective-permute-done.2.refs_0_
  210.3 6.2 %shard_map.72 = (bf16[12,12,128,1024]{3,2,1,0:T(8,128)(2,1)}, bf16[12,12,128,1024]{3,2,1,0:T(8,128)(2,1)}, bf16[2,4,2,12,128,128]{5,4,3,2,1,0:T(8,128)(2,1)S(1)}...) custom-call(bf16[4,128,1024]{2,1,0:T(8,128)(2,1)} %collective-permut, ...), custom_call_target="tpu_custom_call", output_to_operand_aliasing={{3}: (1, {}), {4}: (2, {}), {0}: (3, {}), {1}: (4, {}), {2}... | custom-call | flops 524288 | bytes 524288 | tf_op jit(solution)/shard_map/pallas_call | solution.py:234
Async XLA Ops:
  3.3 6.7 %collective-permute-start.19 = (bf16[4,128,1024]{2,1,0:T(8,128)(2,1)S(1)}, bf16[4,128,1024]{2,1,0:T(8,128)(2,1)S(1)}, u32[]{:S(2)}, u32[]{:S(2)}) collective-permute-start(bf16[4,128,1024]{2,1,0:T(8,128)(2,1)S(1)} %get-tuple-element.63.refs_1_), channel_id=1, source_target_pairs={{0,1},{1,0},{2,3},{3,2},{4,5},{5,4},{6,7},{7,6},{8,9},{9,8},{10,11... | collective-permute-start | bytes 3145736 | tf_op jit(solution)/shard_map/ppermute | solution.py:288
  4.1 8.1 %collective-permute-start.20 = (bf16[4,128,1024]{2,1,0:T(8,128)(2,1)S(1)}, bf16[4,128,1024]{2,1,0:T(8,128)(2,1)S(1)}, u32[]{:S(2)}, u32[]{:S(2)}) collective-permute-start(bf16[4,128,1024]{2,1,0:T(8,128)(2,1)S(1)} %get-tuple-element.62.refs_2_), channel_id=1, source_target_pairs={{0,1},{1,0},{2,3},{3,2},{4,5},{5,4},{6,7},{7,6},{8,9},{9,8},{10,11... | collective-permute-start | bytes 3145736 | tf_op jit(solution)/shard_map/ppermute | solution.py:288
  5.8 25.3 %collective-permute-start.6 = (bf16[4,128,1024]{2,1,0:T(8,128)(2,1)S(1)}, bf16[4,128,1024]{2,1,0:T(8,128)(2,1)S(1)}, u32[]{:S(2)}, u32[]{:S(2)}) collective-permute-start(bf16[4,128,1024]{2,1,0:T(8,128)(2,1)S(1)} %shard_map.60.refs_0_), channel_id=1, source_target_pairs={{0,2},{1,7},{2,4},{3,1},{4,6},{5,3},{6,0},{7,5},{8,10},{9,15},{10,... | collective-permute-start | bytes 3145736 | tf_op jit(solution)/shard_map/ppermute | solution.py:288
  9.5 25.0 %collective-permute-start.18 = (bf16[4,128,1024]{2,1,0:T(8,128)(2,1)S(1)}, bf16[4,128,1024]{2,1,0:T(8,128)(2,1)S(1)}, u32[]{:S(2)}, u32[]{:S(2)}) collective-permute-start(bf16[4,128,1024]{2,1,0:T(8,128)(2,1)S(1)} %shard_map.60.refs_0_), channel_id=1, source_target_pairs={{0,1},{1,0},{2,3},{3,2},{4,5},{5,4},{6,7},{7,6},{8,9},{9,8},{10,11... | collective-permute-start | bytes 3145736 | tf_op jit(solution)/shard_map/ppermute | solution.py:288
  9.5 26.4 %collective-permute-start.15 = (bf16[4,128,1024]{2,1,0:T(8,128)(2,1)S(1)}, bf16[4,128,1024]{2,1,0:T(8,128)(2,1)S(1)}, u32[]{:S(2)}, u32[]{:S(2)}) collective-permute-start(bf16[4,128,1024]{2,1,0:T(8,128)(2,1)S(1)} %shard_map.60.refs_0_), channel_id=1, source_target_pairs={{0,6},{1,3},{2,0},{3,5},{4,2},{5,7},{6,4},{7,1},{8,14},{9,11},{10,... | collective-permute-start | bytes 3145736 | tf_op jit(solution)/shard_map/ppermute | solution.py:288
  10.0 43.6 %collective-permute-start.3 = (bf16[4,128,1024]{2,1,0:T(8,128)(2,1)S(1)}, bf16[4,128,1024]{2,1,0:T(8,128)(2,1)S(1)}, u32[]{:S(2)}, u32[]{:S(2)}) collective-permute-start(bf16[4,128,1024]{2,1,0:T(8,128)(2,1)S(1)} %get-tuple-element.63.refs_1_), channel_id=1, source_target_pairs={{0,2},{1,7},{2,4},{3,1},{4,6},{5,3},{6,0},{7,5},{8,10},{9,15},{10,... | collective-permute-start | bytes 3145736 | tf_op jit(solution)/shard_map/ppermute | solution.py:288
  12.2 46.2 %collective-permute-start.11 = (bf16[4,128,1024]{2,1,0:T(8,128)(2,1)S(1)}, bf16[4,128,1024]{2,1,0:T(8,128)(2,1)S(1)}, u32[]{:S(2)}, u32[]{:S(2)}) collective-permute-start(bf16[4,128,1024]{2,1,0:T(8,128)(2,1)S(1)} %get-tuple-element.63.refs_1_), channel_id=1, source_target_pairs={{0,6},{1,3},{2,0},{3,5},{4,2},{5,7},{6,4},{7,1},{8,14},{9,11},{10,... | collective-permute-start | bytes 3145736 | tf_op jit(solution)/shard_map/ppermute | solution.py:288
  31.1 44.9 %collective-permute-start = (bf16[4,128,1024]{2,1,0:T(8,128)(2,1)S(1)}, bf16[4,128,1024]{2,1,0:T(8,128)(2,1)S(1)}, u32[]{:S(2)}, u32[]{:S(2)}) collective-permute-start(bf16[4,128,1024]{2,1,0:T(8,128)(2,1)S(1)} %get-tuple-element.62.refs_2_), channel_id=1, source_target_pairs={{0,2},{1,7},{2,4},{3,1},{4,6},{5,3},{6,0},{7,5},{8,10},{9,15},{10,... | collective-permute-start | bytes 3145736 | tf_op jit(solution)/shard_map/ppermute | solution.py:288
  34.5 44.1 %collective-permute-start.9 = (bf16[4,128,1024]{2,1,0:T(8,128)(2,1)S(1)}, bf16[4,128,1024]{2,1,0:T(8,128)(2,1)}, u32[]{:S(2)}, u32[]{:S(2)}) collective-permute-start(bf16[4,128,1024]{2,1,0:T(8,128)(2,1)S(1)} %get-tuple-element.62.refs_2_), channel_id=1, source_target_pairs={{0,6},{1,3},{2,0},{3,5},{4,2},{5,7},{6,4},{7,1},{8,14},{9,11},{10,... | collective-permute-start | bytes 3145736 | tf_op jit(solution)/shard_map/ppermute | solution.py:288
  35.9 44.8 %collective-permute-start.17 = (bf16[4,128,1024]{2,1,0:T(8,128)(2,1)S(1)}, bf16[4,128,1024]{2,1,0:T(8,128)(2,1)S(1)}, u32[]{:S(2)}, u32[]{:S(2)}) collective-permute-start(bf16[4,128,1024]{2,1,0:T(8,128)(2,1)S(1)} %collective-permute-done.6.refs_3_), channel_id=1, source_target_pairs={{0,1},{1,0},{2,3},{3,2},{4,5},{5,4},{6,7},{7,6},{8,9},{9,8},{10,11... | collective-permute-start | bytes 3145736 | tf_op jit(solution)/shard_map/ppermute | solution.py:288
  53.6 27.2 %collective-permute-start.16 = (bf16[4,128,1024]{2,1,0:T(8,128)(2,1)S(1)}, bf16[4,128,1024]{2,1,0:T(8,128)(2,1)S(1)}, u32[]{:S(2)}, u32[]{:S(2)}) collective-permute-start(bf16[4,128,1024]{2,1,0:T(8,128)(2,1)S(1)} %collective-permute-done.15.refs_1_), channel_id=1, source_target_pairs={{0,1},{1,0},{2,3},{3,2},{4,5},{5,4},{6,7},{7,6},{8,9},{9,8},{10,11... | collective-permute-start | bytes 3145736 | tf_op jit(solution)/shard_map/ppermute | solution.py:288
  58.4 22.6 %collective-permute-start.14 = (bf16[4,128,1024]{2,1,0:T(8,128)(2,1)S(1)}, bf16[4,128,1024]{2,1,0:T(8,128)(2,1)S(1)}, u32[]{:S(2)}, u32[]{:S(2)}) collective-permute-start(bf16[4,128,1024]{2,1,0:T(8,128)(2,1)S(1)} %collective-permute-done.3.refs_1_), channel_id=1, source_target_pairs={{0,1},{1,0},{2,3},{3,2},{4,5},{5,4},{6,7},{7,6},{8,9},{9,8},{10,11... | collective-permute-start | bytes 3145736 | tf_op jit(solution)/shard_map/ppermute | solution.py:288
  76.0 7.0 %collective-permute-start.13 = (bf16[4,128,1024]{2,1,0:T(8,128)(2,1)S(1)}, bf16[4,128,1024]{2,1,0:T(8,128)(2,1)S(1)}, u32[]{:S(2)}, u32[]{:S(2)}) collective-permute-start(bf16[4,128,1024]{2,1,0:T(8,128)(2,1)S(1)} %collective-permute-done.refs_1_), channel_id=1, source_target_pairs={{0,1},{1,0},{2,3},{3,2},{4,5},{5,4},{6,7},{7,6},{8,9},{9,8},{10,11... | collective-permute-start | bytes 3145736 | tf_op jit(solution)/shard_map/ppermute | solution.py:288
  78.6 14.0 %collective-permute-start.7 = (bf16[4,128,1024]{2,1,0:T(8,128)(2,1)S(1)}, bf16[4,128,1024]{2,1,0:T(8,128)(2,1)}, u32[]{:S(2)}, u32[]{:S(2)}) collective-permute-start(bf16[4,128,1024]{2,1,0:T(8,128)(2,1)S(1)} %collective-permute-done.6.refs_3_), channel_id=1, source_target_pairs={{0,2},{1,7},{2,4},{3,1},{4,6},{5,3},{6,0},{7,5},{8,10},{9,15},{10,... | collective-permute-start | bytes 3145736 | tf_op jit(solution)/shard_map/ppermute | solution.py:288
  80.7 23.1 %collective-permute-start.4 = (bf16[4,128,1024]{2,1,0:T(8,128)(2,1)S(1)}, bf16[4,128,1024]{2,1,0:T(8,128)(2,1)}, u32[]{:S(2)}, u32[]{:S(2)}) collective-permute-start(bf16[4,128,1024]{2,1,0:T(8,128)(2,1)S(1)} %collective-permute-done.3.refs_1_), channel_id=1, source_target_pairs={{0,2},{1,7},{2,4},{3,1},{4,6},{5,3},{6,0},{7,5},{8,10},{9,15},{10,... | collective-permute-start | bytes 3145736 | tf_op jit(solution)/shard_map/ppermute | solution.py:288
  80.8 34.3 %collective-permute-start.1 = (bf16[4,128,1024]{2,1,0:T(8,128)(2,1)S(1)}, bf16[4,128,1024]{2,1,0:T(8,128)(2,1)}, u32[]{:S(2)}, u32[]{:S(2)}) collective-permute-start(bf16[4,128,1024]{2,1,0:T(8,128)(2,1)S(1)} %collective-permute-done.refs_1_), channel_id=1, source_target_pairs={{0,2},{1,7},{2,4},{3,1},{4,6},{5,3},{6,0},{7,5},{8,10},{9,15},{10,... | collective-permute-start | bytes 3145736 | tf_op jit(solution)/shard_map/ppermute | solution.py:288
  80.9 84.7 %collective-permute-start.12 = (bf16[4,128,1024]{2,1,0:T(8,128)(2,1)S(1)}, bf16[4,128,1024]{2,1,0:T(8,128)(2,1)S(1)}, u32[]{:S(2)}, u32[]{:S(2)}) collective-permute-start(bf16[4,128,1024]{2,1,0:T(8,128)(2,1)S(1)} %collective-permute-done.11.refs_1_), channel_id=1, source_target_pairs={{0,1},{1,0},{2,3},{3,2},{4,5},{5,4},{6,7},{7,6},{8,9},{9,8},{10,11... | collective-permute-start | bytes 3145736 | tf_op jit(solution)/shard_map/ppermute | solution.py:288
  83.1 99.5 %collective-permute-start.10 = (bf16[4,128,1024]{2,1,0:T(8,128)(2,1)}, bf16[4,128,1024]{2,1,0:T(8,128)(2,1)}, u32[]{:S(2)}, u32[]{:S(2)}) collective-permute-start(bf16[4,128,1024]{2,1,0:T(8,128)(2,1)} %collective-permute-done.9.refs_0_), channel_id=1, source_target_pairs={{0,1},{1,0},{2,3},{3,2},{4,5},{5,4},{6,7},{7,6},{8,9},{9,8},{10,11... | collective-permute-start | bytes 3145736 | tf_op jit(solution)/shard_map/ppermute | solution.py:288
  92.6 98.4 %collective-permute-start.8 = (bf16[4,128,1024]{2,1,0:T(8,128)(2,1)}, bf16[4,128,1024]{2,1,0:T(8,128)(2,1)}, u32[]{:S(2)}, u32[]{:S(2)}) collective-permute-start(bf16[4,128,1024]{2,1,0:T(8,128)(2,1)} %collective-permute-done.7.refs_1_), channel_id=1, source_target_pairs={{0,1},{1,0},{2,3},{3,2},{4,5},{5,4},{6,7},{7,6},{8,9},{9,8},{10,11... | collective-permute-start | bytes 3145736 | tf_op jit(solution)/shard_map/ppermute | solution.py:288
  103.9 95.7 %collective-permute-start.5 = (bf16[4,128,1024]{2,1,0:T(8,128)(2,1)}, bf16[4,128,1024]{2,1,0:T(8,128)(2,1)}, u32[]{:S(2)}, u32[]{:S(2)}) collective-permute-start(bf16[4,128,1024]{2,1,0:T(8,128)(2,1)} %collective-permute-done.4.refs_1_), channel_id=1, source_target_pairs={{0,1},{1,0},{2,3},{3,2},{4,5},{5,4},{6,7},{7,6},{8,9},{9,8},{10,11... | collective-permute-start | bytes 3145736 | tf_op jit(solution)/shard_map/ppermute | solution.py:288
  115.1 95.2 %collective-permute-start.2 = (bf16[4,128,1024]{2,1,0:T(8,128)(2,1)}, bf16[4,128,1024]{2,1,0:T(8,128)(2,1)}, u32[]{:S(2)}, u32[]{:S(2)}) collective-permute-start(bf16[4,128,1024]{2,1,0:T(8,128)(2,1)} %collective-permute-done.1.refs_0_), channel_id=1, source_target_pairs={{0,1},{1,0},{2,3},{3,2},{4,5},{5,4},{6,7},{7,6},{8,9},{9,8},{10,11... | collective-permute-start | bytes 3145736 | tf_op jit(solution)/shard_map/ppermute | solution.py:288
